TPU v7x, 128 devices: a whole 4x4x4 slice. The times are simulated.
128 devices in a mesh: grp: 4 (over z), seq: 32 (over x, y, core).
Axes of the slice: x: 4, y: 4, z: 4, core: 2. Of those that a mesh axis runs over, the one named last changes fastest.
Arguments:
- stream: bfloat16 [16384, 2048], P(('grp', 'seq')), may hold values from -64 to 64
- cotangent: bfloat16 [16384, 2048], P(('grp', 'seq')), may hold values from -6 to 6
- norm_gain: float32 [2048], replicated, may hold values from 0.5 to 1.5
- queries: bfloat16 [16384, 2048], P(('grp', 'seq')), may hold values from -6 to 6
- key_vectors: bfloat16 [16384, 2048], P(('grp', 'seq')), may hold values from -6 to 6
- value_vectors: bfloat16 [16384, 2048], P(('grp', 'seq')), may hold values from -6 to 6
- expert_index: int32 [128, 256], replicated, may hold values from 0 to 16383, as said below
- router_gates: float32 [128, 256], P(('grp', 'seq')), may hold values from 0.05 to 1
- gate_proj: bfloat16 [128, 2048, 768], P(('grp', 'seq')), may hold values from -0.125 to 0.125
- up_proj: bfloat16 [128, 2048, 768], P(('grp', 'seq')), may hold values from -0.125 to 0.125
- down_proj: bfloat16 [128, 768, 2048], P(('grp', 'seq')), may hold values from -0.21875 to 0.21875
Outputs:
- grad_stream: bfloat16 [16384, 2048], P(('grp', 'seq'))
- grad_queries: bfloat16 [16384, 2048], P(('grp', 'seq'))
- grad_keys: bfloat16 [16384, 2048], P(('grp', 'seq'))
- grad_values: bfloat16 [16384, 2048], P(('grp', 'seq'))
- grad_gate: bfloat16 [128, 2048, 768], P(('grp', 'seq'))
- grad_up: bfloat16 [128, 2048, 768], P(('grp', 'seq'))
- grad_down: bfloat16 [128, 768, 2048], P(('grp', 'seq'))
- grad_router: float32 [128, 256], P(('grp', 'seq'))
- grad_norm_gain: float32 [2048], replicated
Inputs may be any that keep to these rules, and one draw needn't show every extreme that they name: `expert_index`: row e holds 256 different token numbers. Of the 128 tokens numbered d * 128 to (d + 1) * 128 - 1, one expert chooses at most 4, and in every row some d has exactly 4 chosen.
All inputs are finite; a program needn't handle non-finite values.
Results may differ from a plain program's by a relative error of at most 0.024.
Values may be sent and summed in bfloat16 or wider, within the bound.
A program may use at most 192 MiB of HBM per device.

v0:
```python
import math

import jax
import jax.numpy as jnp
from jax import lax
from jax.sharding import Mesh
from jax.sharding import PartitionSpec as P

HEADS = 16
HEAD = 128
BLOCK = 128
SEQ = ("seq_0", "seq_1", "seq_2")
GRP_SEQ = ("grp", "seq_0", "seq_1", "seq_2")


EPS = 1e-06


def one_axis_at_a_time(shard, axes):
    for axis in axes:
        shard = lax.psum(shard, axis)
    return shard


def nothing_yet(shard, identity):
    return jnp.zeros_like(shard) + jnp.asarray(identity, shard.dtype)


def entering(shard, axes, combine, identity):
    before = start = nothing_yet(shard, identity)
    subtotal = shard
    for axis in reversed(axes):
        peers, index = (lax.axis_size(axis), lax.axis_index(axis))
        pieces = lax.all_gather(subtotal.astype(jnp.bfloat16), axis)
        inside, subtotal = (start, start)
        for k in range(peers):
            passed = k < index
            subtotal = combine(subtotal, pieces[k].astype(shard.dtype))
            inside = jnp.where(passed, subtotal, inside)
        before = combine(inside, before)
    return before


def prefix(shard, axis, join, neutral):
    count = lax.axis_size(axis)
    place = lax.axis_index(axis)
    ahead = count - 1 - place
    gathered = lax.all_gather(shard.astype(jnp.bfloat16), axis)
    state = jnp.zeros_like(shard) + jnp.asarray(neutral, shard.dtype)

    def one(hop, state):
        source = count - 1 - hop
        return join(state, lax.dynamic_index_in_dim(gathered, source, 0, False).astype(shard.dtype))

    return lax.fori_loop(0, ahead, one, state)


def expert_back(rows, dy_rows, gates, w_gate, w_up, w_down):
    gate_pre = jnp.dot(rows, w_gate, preferred_element_type=jnp.float32)
    up_pre = jnp.dot(rows, w_up, preferred_element_type=jnp.float32)
    sigmoid_gate = jax.nn.sigmoid(gate_pre)
    silu_gate = gate_pre * sigmoid_gate
    hidden = (silu_gate * up_pre).astype(jnp.bfloat16)
    expert_out = jnp.dot(hidden, w_down, preferred_element_type=jnp.float32)
    grad_router = jnp.sum(dy_rows.astype(jnp.float32) * expert_out, axis=1)
    grad_out = (gates[:, None] * dy_rows.astype(jnp.float32)).astype(jnp.bfloat16)
    grad_down = jnp.dot(hidden.T, grad_out, preferred_element_type=jnp.float32).astype(jnp.bfloat16)
    grad_hidden = jnp.dot(grad_out, w_down.T, preferred_element_type=jnp.float32)
    slope = sigmoid_gate * (1.0 + gate_pre * (1.0 - sigmoid_gate))
    grad_gate_pre = (grad_hidden * up_pre * slope).astype(jnp.bfloat16)
    grad_up_pre = (grad_hidden * silu_gate).astype(jnp.bfloat16)
    grad_gate = jnp.dot(rows.T, grad_gate_pre, preferred_element_type=jnp.float32).astype(
        jnp.bfloat16
    )
    grad_up = jnp.dot(rows.T, grad_up_pre, preferred_element_type=jnp.float32).astype(jnp.bfloat16)
    grad_rows = (
        jnp.dot(grad_gate_pre, w_gate.T, preferred_element_type=jnp.float32)
        + jnp.dot(grad_up_pre, w_up.T, preferred_element_type=jnp.float32)
    ).astype(jnp.bfloat16)
    return (grad_rows, grad_gate, grad_up, grad_down, grad_router)


def add_states(earlier, later):
    return earlier + later


def body(
    stream,
    cotangent,
    norm_gain,
    queries,
    key_vectors,
    value_vectors,
    expert_index,
    router_gates,
    gate_proj,
    up_proj,
    down_proj,
):
    tok_rows, width = stream.shape
    seq_count = lax.axis_size(SEQ)
    grp_count = lax.axis_size("grp")
    dev_count = seq_count * grp_count
    capacity = expert_index.shape[1]
    most = 2 * capacity // dev_count
    here = lax.axis_index("grp") * seq_count + lax.axis_index(SEQ)
    wide_stream = stream.astype(jnp.float32)
    inverse_rms = lax.rsqrt(jnp.mean(wide_stream * wide_stream, axis=1, keepdims=True) + EPS)
    normed = wide_stream * inverse_rms
    inputs = (normed * norm_gain[None, :]).astype(jnp.bfloat16)
    source = expert_index // tok_rows
    mine = (source == here).astype(jnp.int32)
    before_mine = jnp.cumsum(mine, axis=1) - mine
    local_token = expert_index - here * tok_rows
    slot_ids = jnp.arange(most)
    matched = (mine[:, :, None] == 1) & (before_mine[:, :, None] == slot_ids[None, None, :])
    picked = jnp.sum(jnp.where(matched, local_token[:, :, None], 0), axis=1)
    filled = jnp.any(matched, axis=1)
    outgoing = jnp.concatenate([inputs[picked], cotangent[picked]], axis=1)
    incoming = lax.all_to_all(outgoing, GRP_SEQ, split_axis=0, concat_axis=0, tiled=True)
    own_index = lax.dynamic_index_in_dim(expert_index, here, 0, keepdims=False)
    anchor = own_index // tok_rows
    positions = jnp.arange(capacity)
    earlier = jnp.sum(
        (anchor[None, :] == anchor[:, None]) & (positions[None, :] < positions[:, None]), axis=1
    )
    table = incoming.reshape(dev_count * 2 * most, width)
    flat_slot = anchor * (2 * most) + earlier
    grad_rows, grad_gate, grad_up, grad_down, grad_router = expert_back(
        table[flat_slot],
        table[flat_slot + most],
        router_gates[0],
        gate_proj[0],
        up_proj[0],
        down_proj[0],
    )
    back_rows = (
        jnp.zeros((dev_count * most, width), jnp.bfloat16)
        .at[anchor * most + earlier]
        .set(grad_rows)
    )
    returned = lax.all_to_all(
        back_rows.reshape(dev_count, most, width), GRP_SEQ, split_axis=0, concat_axis=0, tiled=True
    )
    returned = returned.reshape(dev_count * most, width)
    combine_table = (
        (jnp.arange(tok_rows)[:, None] == picked.reshape(-1)[None, :]) & filled.reshape(-1)[None, :]
    ).astype(jnp.bfloat16)
    grad_inputs = jnp.dot(combine_table, returned, preferred_element_type=jnp.float32)
    grad_norm_gain = one_axis_at_a_time(jnp.sum(grad_inputs * normed, axis=0), GRP_SEQ)
    grad_normed = grad_inputs * norm_gain[None, :]
    grad_wide = cotangent.astype(jnp.float32) + inverse_rms * (
        grad_normed - normed * jnp.mean(grad_normed * normed, axis=1, keepdims=True)
    )
    grad_stream = grad_wide.astype(jnp.bfloat16)
    blocks = tok_rows // BLOCK
    scale = 1.0 / math.sqrt(HEAD * tok_rows * seq_count)

    def shaped(values):
        return values.reshape(blocks, BLOCK, HEADS, HEAD)

    qq, kk, vv, gg = (
        shaped(queries),
        shaped(key_vectors),
        shaped(value_vectors),
        shaped(grad_stream),
    )
    lower = jnp.arange(BLOCK)[:, None] >= jnp.arange(BLOCK)[None, :]
    mix_a = jnp.where(
        lower, jnp.einsum("ntha,nsha->nhts", gg, vv, preferred_element_type=jnp.float32), 0.0
    ).astype(jnp.bfloat16)
    mix_b = jnp.where(
        lower, jnp.einsum("ntha,nsha->nhts", qq, kk, preferred_element_type=jnp.float32), 0.0
    ).astype(jnp.bfloat16)
    inc_state = jnp.einsum("nsha,nshb->nhab", kk, vv, preferred_element_type=jnp.float32)
    inc_grad = jnp.einsum("ntha,nthb->nhab", qq, gg, preferred_element_type=jnp.float32)
    dev_state = jnp.sum(inc_state, axis=0)
    dev_grad = jnp.sum(inc_grad, axis=0)
    before_dev = entering(dev_state, SEQ, add_states, jnp.zeros_like(dev_state))
    after_dev = prefix(dev_grad, SEQ, add_states, jnp.zeros_like(dev_grad))
    prior_state = before_dev[None] + jnp.cumsum(inc_state, axis=0) - inc_state
    later_state = after_dev[None] + jnp.cumsum(inc_grad[::-1], axis=0)[::-1] - inc_grad
    high = lax.Precision.HIGHEST
    wide_grad = gg.astype(jnp.float32)
    grad_q = scale * (
        jnp.einsum("nhts,nsha->ntha", mix_a, kk, preferred_element_type=jnp.float32)
        + jnp.einsum("nthb,nhab->ntha", wide_grad, prior_state, precision=high)
    )
    grad_k = scale * (
        jnp.einsum("nhts,ntha->nsha", mix_a, qq, preferred_element_type=jnp.float32)
        + jnp.einsum("nshb,nhab->nsha", vv.astype(jnp.float32), later_state, precision=high)
    )
    grad_v = scale * (
        jnp.einsum("nhts,nthb->nshb", mix_b, gg, preferred_element_type=jnp.float32)
        + jnp.einsum("nsha,nhab->nshb", kk.astype(jnp.float32), later_state, precision=high)
    )
    grad_queries = grad_q.reshape(tok_rows, width).astype(jnp.bfloat16)
    grad_keys = grad_k.reshape(tok_rows, width).astype(jnp.bfloat16)
    grad_values = grad_v.reshape(tok_rows, width).astype(jnp.bfloat16)
    return (
        grad_stream,
        grad_queries,
        grad_keys,
        grad_values,
        grad_gate[None],
        grad_up[None],
        grad_down[None],
        grad_router[None],
        grad_norm_gain,
    )


def solution(mesh):
    split = Mesh(
        mesh.devices.reshape(mesh.shape["grp"], 4, 4, 2), ("grp", "seq_0", "seq_1", "seq_2")
    )
    placed = (
        P(GRP_SEQ, None),
        P(GRP_SEQ, None),
        P(),
        P(GRP_SEQ, None),
        P(GRP_SEQ, None),
        P(GRP_SEQ, None),
        P(),
        P(GRP_SEQ, None),
        P(GRP_SEQ, None, None),
        P(GRP_SEQ, None, None),
        P(GRP_SEQ, None, None),
    )
    return jax.shard_map(
        body,
        mesh=split,
        in_specs=placed,
        out_specs=(
            P(GRP_SEQ, None),
            P(GRP_SEQ, None),
            P(GRP_SEQ, None),
            P(GRP_SEQ, None),
            P(GRP_SEQ, None, None),
            P(GRP_SEQ, None, None),
            P(GRP_SEQ, None, None),
            P(GRP_SEQ, None),
            P(),
        ),
        check_vma=False,
    )
```

profile of v0, /device:TPU:0, one launch (start us, length us, event | category | flops | bytes accessed | tf_op | source)
XLA Modules:
  0.0 316.7 jit_solution(9266194692867111362)
XLA Ops:
  12.0 2.0 fusion.42
  14.1 6.3 %gather_fusion = bf16[512,2048]{1,0:T(8,128)(2,1)} fusion(bf16[128,2048]{1,0:T(8,128)(2,1)} %fusion.42, s32[1024]{0:T(1024)S(1)} %pad_clamp_fusion.2), kind=kCustom, calls=%fused_computation | custom fusion | bytes 4196352 | tf_op jit(solution)/shard_map/gather | solution.py:119
  20.4 4.1 %reshape.382 = bf16[128,4,2048]{2,1,0:T(4,128)(2,1)} reshape(bf16[512,2048]{1,0:T(8,128)(2,1)} %gather_fusion) | data formatting | bytes 4194304 | tf_op jit(solution)/shard_map/gather | solution.py:119
  24.5 6.3 %gather_fusion.1 = bf16[512,2048]{1,0:T(8,128)(2,1)} fusion(bf16[128,2048]{1,0:T(8,128)(2,1)} %param.14, s32[1024]{0:T(1024)S(1)} %pad_clamp_fusion.2), kind=kCustom, calls=%fused_computation.1 | custom fusion | bytes 4196352 | tf_op jit(solution)/shard_map/gather | solution.py:119
  30.8 4.1 %reshape.390 = bf16[128,4,2048]{2,1,0:T(4,128)(2,1)} reshape(bf16[512,2048]{1,0:T(8,128)(2,1)} %gather_fusion.1) | data formatting | bytes 4194304 | tf_op jit(solution)/shard_map/gather | solution.py:119
  34.9 5.1 %pad_maximum_fusion = bf16[128,8,2048]{2,1,0:T(8,128)(2,1)} fusion(bf16[128,4,2048]{2,1,0:T(4,128)(2,1)} %reshape.390, bf16[128,4,2048]{2,1,0:T(4,128)(2,1)} %reshape.382), kind=kLoop, calls=%fused_computation.6 | loop fusion | flops 8388608 | bytes 8388608 | tf_op jit(solution)/shard_map/concatenate | solution.py:119
  40.0 11.7 %all-to-all-start = ((bf16[128,8,2048]{2,1,0:T(8,128)(2,1)}), bf16[128,8,2048]{2,1,0:T(8,128)(2,1)}, u32[]{:S(2)}, u32[]{:S(2)}) async-start(bf16[128,8,2048]{2,1,0:T(8,128)(2,1)} %pad_maximum_fusion), calls=%async_computation | async-start | bytes 8388608 | tf_op jit(solution)/shard_map/all_to_all | solution.py:120
  51.7 2.7 fusion.141
  54.7 12.8 %all-gather.11.cloned.1.call-done = bf16[32,128,128]{2,1,0:T(8,128)(2,1)} async-done(((bf16[16,128,128]{2,1,0:T(8,128)(2,1)}), bf16[32,128,128]{2,1,0:T(8,128)(2,1)}) %all-gather.11.cloned.1.call-update) | async-done | bytes 1048592 | tf_op jit(solution)/shard_map/all_gather | solution.py:34
  67.5 2.1 fusion.71
  69.9 34.3 %all-to-all-done = bf16[128,8,2048]{2,1,0:T(8,128)(2,1)} async-done(((bf16[128,8,2048]{2,1,0:T(8,128)(2,1)}), bf16[128,8,2048]{2,1,0:T(8,128)(2,1)}, u32[]{:S(2)}, u32[]{:S(2)}) %all-to-all-start) | async-done | bytes 4194336 | tf_op jit(solution)/shard_map/all_to_all | solution.py:120
  104.2 6.1 %gather_fusion.2 = bf16[256,2048]{1,0:T(8,128)(2,1)} fusion(bf16[1024,2048]{1,0:T(8,128)(2,1)} %bitcast.11, s32[1024]{0:T(1024)S(1)} %pad_clamp_fusion.1), kind=kCustom, calls=%fused_computation.2 | custom fusion | bytes 2098176 | tf_op jit(solution)/shard_map/gather | solution.py:131
  110.3 6.1 %gather_fusion.3 = bf16[256,2048]{1,0:T(8,128)(2,1)} fusion(bf16[1024,2048]{1,0:T(8,128)(2,1)} %bitcast.11, s32[1024]{0:T(1024)S(1)} %pad_clamp_fusion), kind=kCustom, calls=%fused_computation.3 | custom fusion | bytes 2098176 | tf_op jit(solution)/shard_map/gather | solution.py:130
  116.4 3.3 %fusion.2 = f32[256,768]{1,0:T(8,128)S(1)} fusion(bf16[256,2048]{1,0:T(8,128)(2,1)} %gather_fusion.3, bf16[1,2048,768]{2,1,0:T(8,128)(2,1)} %param.21), kind=kOutput, calls=%fused_computation.12 | convolution fusion | flops 805306368 | bytes 4980736 | tf_op jit(solution)/shard_map/dot_general | solution.py:59
  121.1 2.0 multiply_convert_fusion
  124.1 2.0 fusion.21
  126.1 3.7 %scatter_custom_fusion = bf16[512,2048]{1,0:T(8,128)(2,1)S(1)} fusion(s32[256]{0:T(256)S(1)} %bitcast.208, bf16[256,2048]{1,0:T(8,128)(2,1)} %fusion.21, bf16[]{:T(256)} %constant.109.clone.1), kind=kCustom, calls=%fused_computation.90 | custom fusion | bytes 2097664 | tf_op jit(solution)/shard_map/scatter | solution.py:140
  129.9 2.2 reshape.368
  132.1 7.2 %all-to-all-start.1 = ((bf16[128,4,2048]{2,1,0:T(4,128)(2,1)}), bf16[128,4,2048]{2,1,0:T(4,128)(2,1)S(1)}, u32[]{:S(2)}, u32[]{:S(2)}) async-start(bf16[128,4,2048]{2,1,0:T(4,128)(2,1)} %reshape.368), calls=%async_computation.1 | async-start | bytes 4194304 | tf_op jit(solution)/shard_map/all_to_all | solution.py:142
  139.3 2.7 fusion.67
  142.8 34.5 %all-to-all-done.1 = bf16[128,4,2048]{2,1,0:T(4,128)(2,1)S(1)} async-done(((bf16[128,4,2048]{2,1,0:T(4,128)(2,1)}), bf16[128,4,2048]{2,1,0:T(4,128)(2,1)S(1)}, u32[]{:S(2)}, u32[]{:S(2)}) %all-to-all-start.1) | async-done | bytes 2097184 | tf_op jit(solution)/shard_map/all_to_all | solution.py:142
  177.3 2.0 reshape.369
  179.3 2.9 fusion.48
  184.7 4.0 %fusion.12 = bf16[1,2048,768]{2,1,0:T(8,128)(2,1)} fusion(bf16[256,2048]{1,0:T(8,128)(2,1)} %gather_fusion.3, bf16[256,768]{1,0:T(8,128)(2,1)S(1)} %copy-done.20), kind=kOutput, calls=%fused_computation.22 | convolution fusion | flops 806879232 | bytes 4587520 | tf_op jit(solution)/shard_map/dot_general | solution.py:72
  188.7 2.7 fusion.13
  191.4 2.8 fusion.14
  194.2 1.6 fusion.25
  195.9 8.8 %psum.28 = f32[2048]{0:T(1024)S(1)} all-reduce(f32[2048]{0:T(1024)S(1)} %copy-done.22), channel_id=1, replica_groups=mesh['grp'=4,'seq_0'=4,'seq_1'=4,'seq_2'=2] {'grp'}, use_global_device_ids=true, to_apply=%region_12.13 | all-reduce | flops 2048 | bytes 16384 | tf_op jit(solution)/shard_map/psum | solution.py:21
  204.7 8.8 %psum.29 = f32[2048]{0:T(1024)S(1)} all-reduce(f32[2048]{0:T(1024)S(1)} %psum.28), channel_id=1, replica_groups=mesh['grp'=4,'seq_0'=4,'seq_1'=4,'seq_2'=2] {'seq_0'}, use_global_device_ids=true, to_apply=%region_13.14 | all-reduce | flops 2048 | bytes 16384 | tf_op jit(solution)/shard_map/psum | solution.py:21
  213.5 8.6 %psum.30 = f32[2048]{0:T(1024)S(1)} all-reduce(f32[2048]{0:T(1024)S(1)} %psum.29), channel_id=1, replica_groups=mesh['grp'=4,'seq_0'=4,'seq_1'=4,'seq_2'=2] {'seq_1'}, use_global_device_ids=true, to_apply=%region_14.15 | all-reduce | flops 2048 | bytes 16384 | tf_op jit(solution)/shard_map/psum | solution.py:21
  222.2 3.1 psum.31
  226.6 1.5 convolution_bitcast_fusion.2
  228.2 1.6 fusion.41
  229.8 5.2 %fusion.39 = bf16[16,128,128]{2,1,0:T(8,128)(2,1)S(1)} fusion(f32[16,128,128]{2,1,0:T(8,128)} %convolution_bitcast_fusion.2, bf16[128,16,128]{0,2,1:T(8,128)(2,1)S(1)} %bitcast.193, f32[16,128,128]{2,1,0:T(8,128)} %get-tuple-element.133, bf16[4,16,128,128]{3,2,1,0:T(8,128)(2,1)} %all-gather.9.cloned.1.call-done, pred[]{:T(512)S(6)} %gt.38, pred[]{:T(512)S(6)} %gt.39, ...), kind=kOutput, calls=%fused_computation.59 | convolution fusion | flops 411566080 | bytes 8388618 | tf_op jit(solution)/shard_map/nthb,nhab->ntha/dot_general | solution.py:187
  236.0 20.7 %all-gather.13.cloned.1.call-done = bf16[512,128,128]{2,1,0:T(8,128)(2,1)} async-done(((bf16[16,128,128]{2,1,0:T(8,128)(2,1)}), bf16[512,128,128]{2,1,0:T(8,128)(2,1)}) %all-gather.13.cloned.1.call-update) | async-done | bytes 16777232 | tf_op jit(solution)/shard_map/all_gather | solution.py:48
  256.8 40.9 %while.12 = (s32[]{:T(128)}, f32[16,128,128]{2,1,0:T(8,128)S(1)}, s32[]{:T(128)}, bf16[32,16,128,128]{3,2,1,0:T(8,128)(2,1)}, s32[]{:T(128)}, /*index=5*/s32[]{:T(128)}, s32[]{:T(128)}, s32[]{:T(128)}) while((s32[]{:T(128)}, f32[16,128,128]{2,1,0:T(8,128)S(1)}, s32[]{:T(128)}, bf16[32,16,128,128]{3,2,1,0:T(8,128)(2,1)}, s32[]{:T(128)}, ...), condition=%wide.region_9.10_spmd, body=%wide.region_8.9_spmd.sunk | while | flops 524294 | bytes 2621575 | solution.py:55
  258.4 1.3 convert_add_fusion.12
  262.3 1.3 convert_add_fusion.12
  263.7 1.3 convert_add_fusion.12
  266.3 1.3 convert_add_fusion.12
  267.6 1.3 convert_add_fusion.12
  270.2 1.3 convert_add_fusion.12
  271.5 1.3 convert_add_fusion.12
  298.1 3.1 fusion.82
  301.2 2.0 fusion.40
  303.2 2.2 copy.123
  305.4 2.7 fusion.36
  308.2 2.0 copy.122
  (134 shorter events, 44.4 us)
Async XLA Ops:
  7.2 113.7 %copy-start = (bf16[1,2048,768]{2,1,0:T(8,128)(2,1)S(1)}, bf16[1,2048,768]{2,1,0:T(8,128)(2,1)}, u32[]{:S(2)}) copy-start(bf16[1,2048,768]{2,1,0:T(8,128)(2,1)} %param.22) | copy-start | bytes 9437188
  7.2 3.2 copy-start.16
  7.2 4.8 %copy-start.21 = (f32[2048]{0:T(1024)S(1)}, f32[2048]{0:T(1024)}, u32[]{:S(2)}) copy-start(f32[2048]{0:T(1024)} %param.15) | copy-start | bytes 24580
  40.0 64.2 %all-to-all-start = ((bf16[128,8,2048]{2,1,0:T(8,128)(2,1)}), bf16[128,8,2048]{2,1,0:T(8,128)(2,1)}, u32[]{:S(2)}, u32[]{:S(2)}) async-start(bf16[128,8,2048]{2,1,0:T(8,128)(2,1)} %pad_maximum_fusion), calls=%async_computation | async-start | bytes 8388608 | tf_op jit(solution)/shard_map/all_to_all | solution.py:120
  51.7 15.8 %all-gather.11.cloned.1.call-start = ((), (), s32[]{:S(2)}) async-start(), calls=%async_computation.4 | async-start | bytes 1572864 | tf_op jit(solution)/shard_map/all_gather | solution.py:34
  54.5 84.9 %all-gather.7.cloned.1.call-start = ((), (), s32[]{:S(2)}) async-start(), calls=%async_computation.2 | async-start | bytes 2621440 | tf_op jit(solution)/shard_map/all_gather | solution.py:34
  116.4 3.3 %copy-start.12 = (bf16[256,2048]{1,0:T(8,128)(2,1)S(1)}, bf16[256,2048]{1,0:T(8,128)(2,1)}, u32[]{:S(2)}) copy-start(bf16[256,2048]{1,0:T(8,128)(2,1)} %gather_fusion.2) | copy-start | bytes 3145732
  116.4 3.5 %copy-start.23 = (bf16[1,768,2048]{2,1,0:T(8,128)(2,1)S(1)}, bf16[1,768,2048]{2,1,0:T(8,128)(2,1)}, u32[]{:S(2)}) copy-start(bf16[1,768,2048]{2,1,0:T(8,128)(2,1)} %param.23) | copy-start | bytes 9437188
  116.4 3.5 %copy-start.25 = (f32[1,256]{1,0:T(1,128)S(1)}, f32[1,256]{1,0:T(1,128)}, u32[]{:S(2)}) copy-start(f32[1,256]{1,0:T(1,128)} %param.20) | copy-start | bytes 3076
  119.9 1.2 copy-start.14
  121.1 2.0 copy-start.8
  123.1 1.0 copy-start.19
  123.1 1.0 copy-start.17
  132.1 45.2 %all-to-all-start.1 = ((bf16[128,4,2048]{2,1,0:T(4,128)(2,1)}), bf16[128,4,2048]{2,1,0:T(4,128)(2,1)S(1)}, u32[]{:S(2)}, u32[]{:S(2)}) async-start(bf16[128,4,2048]{2,1,0:T(4,128)(2,1)} %reshape.368), calls=%async_computation.1 | async-start | bytes 4194304 | tf_op jit(solution)/shard_map/all_to_all | solution.py:142
  139.3 90.5 %all-gather.9.cloned.1.call-start = ((), (), s32[]{:S(2)}) async-start(), calls=%async_computation.3 | async-start | bytes 2621440 | tf_op jit(solution)/shard_map/all_gather | solution.py:34
  142.0 114.7 %all-gather.13.cloned.1.call-start = ((), (), s32[]{:S(2)}) async-start(), calls=%async_computation.5 | async-start | bytes 17301504 | tf_op jit(solution)/shard_map/all_gather | solution.py:48
  142.7 36.5 %copy-start.3 = (bf16[128,2048]{1,0:T(8,128)(2,1)S(1)}, bf16[128,2048]{1,0:T(8,128)(2,1)}, u32[]{:S(2)}) copy-start(bf16[128,2048]{1,0:T(8,128)(2,1)} %param.13) | copy-start | bytes 1572868
  179.3 2.9 copy-start.2
  182.2 1.0 copy-start.6
  182.6 1.9 copy-start.10
  183.2 1.4 copy-start.20
  184.6 4.1 %copy-start.15 = (bf16[256,2048]{1,0:T(8,128)(2,1)S(1)}, bf16[256,2048]{1,0:T(8,128)(2,1)}, u32[]{:S(2)}) copy-start(bf16[256,2048]{1,0:T(8,128)(2,1)} %gather_fusion.3) | copy-start | bytes 3145732
  184.6 4.0 %copy-start.18 = (bf16[256,768]{1,0:T(8,128)(2,1)S(1)}, bf16[256,768]{1,0:T(8,128)(2,1)}, u32[]{:S(2)}) copy-start(bf16[256,768]{1,0:T(8,128)(2,1)} %copy-done.17) | copy-start | bytes 1179652
  188.7 2.7 copy-start.13
  188.7 2.7 copy-start.26
  188.7 2.7 copy-start.27
  191.4 2.8 copy-start.24
  194.2 1.6 copy-start.22
  194.2 31.1 %copy-start.9 = (bf16[128,2048]{1,0:T(8,128)(2,1)S(1)}, bf16[128,2048]{1,0:T(8,128)(2,1)}, u32[]{:S(2)}) copy-start(bf16[128,2048]{1,0:T(8,128)(2,1)} %param.18) | copy-start | bytes 1572868
  194.2 32.4 %copy-start.4 = (bf16[128,2048]{1,0:T(8,128)(2,1)S(1)}, bf16[128,2048]{1,0:T(8,128)(2,1)}, u32[]{:S(2)}) copy-start(bf16[128,2048]{1,0:T(8,128)(2,1)} %param.17) | copy-start | bytes 1572868
  225.8 0.8 copy-start.11
  298.1 3.2 copy-start.5
  298.1 3.2 copy-start.7
  303.2 7.0 %copy-start.1 = (bf16[1,2048,768]{2,1,0:T(8,128)(2,1)S(1)}, bf16[1,2048,768]{2,1,0:T(8,128)(2,1)}, u32[]{:S(2)}) copy-start(bf16[1,2048,768]{2,1,0:T(8,128)(2,1)} %param.22) | copy-start | bytes 9437188
Sparse Core Ops, SparseCore 0:
  54.7 12.6 all-gather.10
  69.8 46.0 all-gather.6
  142.3 39.0 all-gather.8
  184.7 71.9 all-gather.12
where the time goes:
time: 319 us; the launch traced here: 317 us
  waiting for transfers between devices  102 us (32%)
  other arithmetic  54.8 us (17%)
  local copies, waits for them, and re-layouts  52.3 us (16%)
  matrix products  43.1 us (14%)
  blocking collectives  29.4 us (9%)
  starting transfers between devices  19.3 us (6%)
  between operations  14.3 us (4%)
    add x31, other arithmetic, add_states(): return earlier + later  39.8 us
    all_to_all x1, waiting for transfers between devices, body(): lax.all_to_all(back_rows.reshape(dev_count, most, width), GRP_SEQ, split_...  34.5 us
    all_to_all x1, waiting for transfers between devices, body(): lax.all_to_all(outgoing, GRP_SEQ, split_axis=0, concat_axis=0, tiled=True)  34.3 us
    psum x4, blocking collectives, one_axis_at_a_time(): shard = lax.psum(shard, axis)  29.4 us
    gather x4, local copies, waits for them, and re-layouts, body(): outgoing = jnp.concatenate([inputs[picked], cotangent[picked]], axis=1)  20.9 us
    all_gather x1, waiting for transfers between devices, prefix(): gathered = lax.all_gather(shard.astype(jnp.bfloat16), axis)  20.7 us
    all_gather x3, waiting for transfers between devices, entering(): pieces = lax.all_gather(subtotal.astype(jnp.bfloat16), axis)  12.8 us
    all_to_all x1, starting transfers between devices, body(): lax.all_to_all(outgoing, GRP_SEQ, split_axis=0, concat_axis=0, tiled=True)  11.7 us
  transfers between devices with their start and end apart: 6, of which 4 were waited for; matrix products, arithmetic and copies ran while one was open for 20% of the time, Pallas kernels for 0%

commit v1 on v0

v1 whole, which is shorter than its diff:
```python
import functools
import math

import jax
import jax.numpy as jnp
from jax import lax
from jax.experimental import pallas as pl
from jax.experimental.pallas import tpu as pltpu
from jax.sharding import PartitionSpec as P

D = 2048
FF = 768
HEADS = 16
HEAD = 128
CAP = 256
TOK = 128
DEV = 128
PLANE = 32
SLOTS = 4
EPS = 1e-06
MULT = 37
MULT_INV = 45
PLANE_MULT = 13
MESH = pl.DeviceIdType.MESH
BF = jnp.bfloat16
F32 = jnp.float32


def dot(a, b):
    return lax.dot_general(a, b, (((1,), (0,)), ((), ())), preferred_element_type=F32)


def dot_nt(a, b):
    return lax.dot_general(a, b, (((1,), (1,)), ((), ())), preferred_element_type=F32)


def dot_tn(a, b):
    return lax.dot_general(a, b, (((0,), (0,)), ((), ())), preferred_element_type=F32)


def rem(a, n):
    return lax.rem(a, jnp.int32(n))


def div(a, n):
    return lax.div(a, jnp.int32(n))


def offsets(i):
    k = rem(i * MULT, DEV)
    return div(k, 32), rem(div(k, 8), 4), rem(div(k, 2), 4), rem(k, 2)


def index_of(z, x, y, c):
    return rem(z, 4), rem(x, 4) * 8 + rem(y, 4) * 2 + rem(c, 2)


def mega(
    stream_h, cot_h, gain_h, code_h, tcol_h, trow_h, gates_h, wg_h, wu_h, wd_h, q_h, k_h, v_h,
    rows_o, gout_o, hid_o, dgp_o, dup_o, router_o, g_o, prior_o, later_o, gain_o,
    stream, cot, gain, code, tcol, trow, gates, wg, wu, wd, qv, kv, vv,
    normed, xin, p8, send, recv, acc, rows, gout, hid, dgp, dup, stacked, rsend, rrecv,
    gin, g, skv, sqg, kv1, kvs, kv2, qg1, qgs, qg2, gpart, gland, router,
    lsem, osem, fsem, frsem, bsem, brsem, asem, arsem, gsem, grsem, zsem,
):
    z = lax.axis_index("grp")
    s = lax.axis_index("seq")
    x, y, c = div(s, 8), rem(div(s, 2), 4), rem(s, 2)

    def dev(z2, s2):
        return {"grp": z2, "seq": s2}

    def out_to(i):
        dz, dx, dy, dc = offsets(i)
        return dev(*index_of(z + dz, x + dx, y + dy, c + dc))

    def back_to(i):
        dz, dx, dy, dc = offsets(i)
        return dev(*index_of(z + 4 - dz, x + 4 - dx, y + 4 - dy, c + dc))

    def plane_to(j):
        k = rem(j * PLANE_MULT, PLANE)
        return index_of(z, x + div(k, 8), y + rem(div(k, 2), 4), c + rem(k, 2))[1]

    bar = pltpu.get_barrier_semaphore()

    def greet(j, carry):
        pl.semaphore_signal(bar, inc=1, device_id=dev(z, plane_to(j)), device_id_type=MESH)
        return carry

    lax.fori_loop(1, PLANE, greet, 0)
    for d in (1, 2, 3):
        pl.semaphore_signal(bar, inc=1, device_id=dev(rem(z + d, 4), s), device_id_type=MESH)

    loads = [
        (stream_h, stream), (cot_h, cot), (gain_h, gain), (code_h, code), (tcol_h, tcol), (trow_h, trow),
        (gates_h, gates), (q_h, qv), (k_h, kv), (v_h, vv), (wg_h, wg), (wu_h, wu), (wd_h, wd),
    ]
    load = [pltpu.make_async_copy(a, b, lsem.at[n]) for n, (a, b) in enumerate(loads)]
    for cp in load:
        cp.start()

    for n in (0, 1, 2, 3):
        load[n].wait()
    wide = stream[...].astype(F32)
    inv = lax.rsqrt(jnp.mean(wide * wide, axis=1, keepdims=True) + EPS)
    nrm = wide * inv
    normed[...] = nrm
    xin[0:TOK, :] = (nrm * gain[...]).astype(BF)
    xin[TOK:, :] = cot[...]

    def build(gi, carry):
        r = lax.broadcasted_iota(jnp.int32, (256, 128), 0) + gi * 256
        lane = lax.broadcasted_iota(jnp.int32, (256, 128), 1)
        k = ((r >> 3) * MULT) & (DEV - 1)
        e = ((z + (k >> 5)) & 3) * 32 + ((x + (k >> 3)) & 3) * 8 + ((y + (k >> 1)) & 3) * 2 + ((c + k) & 1)
        pick = jnp.where(e == lane, 1.0, 0.0).astype(BF)
        rep = dot(pick, code[...])
        want = ((r & 3) + 1).astype(F32)
        hit = jnp.where(rep == want, 1.0, 0.0)
        kind = (r >> 2) & 1
        row0 = pl.multiple_of(gi * 256, 256)
        p8[pl.ds(row0, 256), 0:128] = jnp.where(kind == 0, hit, 0.0).astype(BF)
        p8[pl.ds(row0, 256), 128:256] = jnp.where(kind == 1, hit, 0.0).astype(BF)
        return carry

    lax.fori_loop(0, 4, build, 0)

    def fill(gi, carry):
        row0 = pl.multiple_of(gi * 256, 256)
        sel = p8[pl.ds(row0, 256), :]
        lo = dot(sel, xin[:, 0:1024]).reshape(32, 8, 1024)
        hi = dot(sel, xin[:, 1024:2048]).reshape(32, 8, 1024)
        send[pl.ds(gi * 32, 32)] = jnp.concatenate([lo, hi], axis=1).astype(BF)
        return carry

    lax.fori_loop(0, 4, fill, 0)

    pl.semaphore_wait(bar, PLANE - 1 + 3)
    for d in (1, 2, 3):
        pl.semaphore_signal(zsem, inc=1, device_id=dev(rem(z + d, 4), s), device_id_type=MESH)
    pl.semaphore_wait(zsem, 3)

    def push(i, carry):
        pltpu.make_async_remote_copy(
            send.at[i], recv.at[i], fsem, frsem.at[div(i, 32)], device_id=out_to(i), device_id_type=MESH
        ).start()
        return carry

    lax.fori_loop(1, DEV, push, 0)
    recv[0] = send[0]

    load[7].wait()
    load[8].wait()
    load[9].wait()
    for h in range(HEADS):
        kh = kv[:, h * HEAD:(h + 1) * HEAD]
        vh = vv[:, h * HEAD:(h + 1) * HEAD]
        skv[2 * h:2 * h + 2] = dot_tn(kh, vh).reshape(2, 64, HEAD).astype(BF)

    load[4].wait()
    load[5].wait()
    load[6].wait()

    acc[...] = jnp.zeros_like(acc)
    for gi in range(4):
        first = 1 if gi == 0 else 0
        span = recv.at[pl.ds(gi * 32 + first, 32 - first)]
        pltpu.make_async_copy(span, span, frsem.at[gi]).wait()
        lane = lax.broadcasted_iota(jnp.int32, (512, 256), 1) + gi * 256
        put = jnp.where(lane == tcol[:, 0:1], 1.0, 0.0).astype(BF)
        for half in range(2):
            f = recv[pl.ds(gi * 32, 32)].astype(F32).reshape(32, 2, 8, 1024)[:, half]
            f = f.reshape(256, 1024).astype(BF)
            acc[:, half * 1024:(half + 1) * 1024] += dot(put, f)

    def scatter(src, dst, sem, rsem):
        def one(j, carry):
            to = plane_to(j)
            pltpu.make_async_remote_copy(
                src.at[to], dst.at[s], sem, rsem, device_id=dev(z, to), device_id_type=MESH
            ).start()
            return carry

        lax.fori_loop(1, PLANE, one, 0)
        dst[s] = src[s]

    def arrived(dst, rsem):
        span = dst.at[pl.ds(0, PLANE - 1)]
        pltpu.make_async_copy(span, span, rsem).wait()

    scatter(skv, kv1, asem.at[0], arsem.at[0])

    rows[...] = acc[0:CAP, :].astype(BF)
    dyf = acc[CAP:, :]
    gout[...] = (gates[:, 0:1] * dyf).astype(BF)
    for n in (10, 11, 12):
        load[n].wait()

    def front(n, carry):
        c0 = pl.multiple_of(n * 256, 256)
        gp = dot(rows[...], wg[:, pl.ds(c0, 256)])
        up = dot(rows[...], wu[:, pl.ds(c0, 256)])
        gh = dot_nt(gout[...], wd[pl.ds(c0, 256), :])
        sg = jax.nn.sigmoid(gp)
        silu = gp * sg
        hid[:, pl.ds(c0, 256)] = (silu * up).astype(BF)
        dgp[:, pl.ds(c0, 256)] = (gh * up * (sg * (1.0 + gp * (1.0 - sg)))).astype(BF)
        dup[:, pl.ds(c0, 256)] = (gh * silu).astype(BF)
        return carry

    lax.fori_loop(0, 3, front, 0)

    def back(n, carry):
        r0 = pl.multiple_of(n * 256, 256)
        gr = dot_nt(dgp[...], wg[pl.ds(r0, 256), :]) + dot_nt(dup[...], wu[pl.ds(r0, 256), :])
        h0 = pl.multiple_of(div(n, 4) * 256, 256)
        c0 = pl.multiple_of(rem(n, 4) * 256, 256)
        stacked[pl.ds(h0, 256), pl.ds(c0, 256)] = gr.astype(BF)
        return carry

    lax.fori_loop(0, 8, back, 0)

    def refill(gi, carry):
        r = lax.broadcasted_iota(jnp.int32, (256, 512), 0) + gi * 256
        put = jnp.where(r == trow[...], 1.0, 0.0).astype(BF)
        o = dot(put, stacked[...]).reshape(32, 8, 1024)
        o = jnp.concatenate([o[:, :, 0:512], o[:, :, 512:1024]], axis=1)
        rsend[pl.ds(gi * 32, 32)] = o.astype(BF)
        return carry

    def ret(i, carry):
        pltpu.make_async_remote_copy(
            rsend.at[i], rrecv.at[i], bsem, brsem.at[div(i, 32)], device_id=back_to(i), device_id_type=MESH
        ).start()
        return carry

    lax.fori_loop(0, 2, refill, 0)
    lax.fori_loop(1, 32, ret, 0)
    lax.fori_loop(2, 3, refill, 0)
    lax.fori_loop(32, 64, ret, 0)
    lax.fori_loop(3, 4, refill, 0)
    lax.fori_loop(64, 128, ret, 0)
    rrecv[0] = rsend[0]

    outs = [(rows, rows_o), (gout, gout_o), (hid, hid_o), (dgp, dgp_o), (dup, dup_o)]
    store = [pltpu.make_async_copy(a, b, osem.at[n]) for n, (a, b) in enumerate(outs)]
    for cp in store:
        cp.start()

    def route(n, total):
        c0 = pl.multiple_of(n * 256, 256)
        eo = dot(hid[...], wd[:, pl.ds(c0, 256)])
        return total + jnp.sum(acc[CAP:, pl.ds(c0, 256)] * eo, axis=1, keepdims=True)

    router[...] = jnp.broadcast_to(lax.fori_loop(0, 8, route, jnp.zeros((CAP, 1), F32)), router.shape)

    arrived(kv1, arsem.at[0])

    def prefix(r, total):
        kvs[r] = total.astype(BF)
        return total + kv1[r].astype(F32)

    lax.fori_loop(0, PLANE, prefix, jnp.zeros((64, HEAD), F32))

    for gi in range(4):
        first = 1 if gi == 0 else 0
        span = rrecv.at[pl.ds(gi * 32 + first, 32 - first)]
        pltpu.make_async_copy(span, span, brsem.at[gi]).wait()
        for half in range(2):
            f = rrecv[pl.ds(gi * 32, 32)].astype(F32).reshape(32, 2, 8, 512)[:, half]
            f = f.reshape(256, 512).astype(BF)
            part = dot_tn(p8[gi * 256:(gi + 1) * 256, :], f)
            for hh in range(2):
                c0 = hh * 1024 + half * 512
                piece = part[hh * TOK:(hh + 1) * TOK, :]
                if gi == 0:
                    gin[:, c0:c0 + 512] = piece
                else:
                    gin[:, c0:c0 + 512] += piece

    scatter(kvs, kv2, asem.at[1], arsem.at[1])

    gi_ = gin[...]
    nrm = normed[...]

    def spread(stage):
        if stage == 0:
            to = [dev(z, s + 1 - 2 * c)]
        elif stage == 1:
            to = [dev(z, x * 8 + rem(y + d, 4) * 2 + c) for d in (1, 2, 3)]
        elif stage == 2:
            to = [dev(z, rem(x + d, 4) * 8 + y * 2 + c) for d in (1, 2, 3)]
        else:
            to = [dev(rem(z + d, 4), s) for d in (1, 2, 3)]
        cps = [
            pltpu.make_async_remote_copy(
                gpart.at[stage], gland.at[stage, d], gsem.at[stage, d], grsem.at[stage, d],
                device_id=t, device_id_type=MESH,
            )
            for d, t in enumerate(to)
        ]
        for cp in cps:
            cp.start()
        return cps

    def collect(stage, cps):
        for cp in cps:
            cp.wait()
        total = gpart[stage]
        for d in range(len(cps)):
            total = total + gland[stage, d]
        return total

    gpart[0] = jnp.sum(gi_ * nrm, axis=0, keepdims=True)
    cps0 = spread(0)

    gn = gi_ * gain[...]
    wide_g = cot[...].astype(F32) + inv * (gn - nrm * jnp.mean(gn * nrm, axis=1, keepdims=True))
    g[...] = wide_g.astype(BF)
    gcp = pltpu.make_async_copy(g, g_o, osem.at[5])
    gcp.start()
    for h in range(HEADS):
        qh = qv[:, h * HEAD:(h + 1) * HEAD]
        gh = g[:, h * HEAD:(h + 1) * HEAD]
        sqg[2 * h:2 * h + 2] = dot_tn(qh, gh).reshape(2, 64, HEAD).astype(BF)
    scatter(sqg, qg1, asem.at[2], arsem.at[2])
    gpart[1] = collect(0, cps0)
    cps1 = spread(1)
    arrived(qg1, arsem.at[2])

    def suffix(n, total):
        r = PLANE - 1 - n
        qgs[r] = total.astype(BF)
        return total + qg1[r].astype(F32)

    lax.fori_loop(0, PLANE, suffix, jnp.zeros((64, HEAD), F32))
    scatter(qgs, qg2, asem.at[3], arsem.at[3])
    gpart[2] = collect(1, cps1)
    cps2 = spread(2)
    arrived(kv2, arsem.at[1])
    pcp = pltpu.make_async_copy(kv2, prior_o, osem.at[6])
    pcp.start()
    gpart[3] = collect(2, cps2)
    cps3 = spread(3)
    arrived(qg2, arsem.at[3])
    lcp = pltpu.make_async_copy(qg2, later_o, osem.at[7])
    lcp.start()
    gpart[4] = collect(3, cps3)
    ncp = pltpu.make_async_copy(gpart.at[4], gain_o, osem.at[8])
    ncp.start()
    rcp = pltpu.make_async_copy(router, router_o, osem.at[9])
    rcp.start()

    span = send.at[pl.ds(1, DEV - 1)]
    pltpu.make_async_copy(span, span, fsem).wait()
    span = rsend.at[pl.ds(1, DEV - 1)]
    pltpu.make_async_copy(span, span, bsem).wait()
    for n, buf in enumerate((skv, kvs, sqg, qgs)):
        arrived(buf, asem.at[n])
    for cp in store + [gcp, pcp, lcp, ncp, rcp]:
        cp.wait()


def call_mega(operands):
    def vm(shape, dtype):
        return pltpu.VMEM(shape, dtype)

    state = (PLANE, 64, HEAD)
    results = [
        ((CAP, D), BF), ((CAP, D), BF), ((CAP, FF), BF), ((CAP, FF), BF), ((CAP, FF), BF), ((CAP, 128), F32),
        ((TOK, D), BF), (state, BF), (state, BF), ((1, D), F32),
    ]
    scratch = [
        vm((TOK, D), BF), vm((TOK, D), BF), vm((1, D), F32), vm((DEV, TOK), BF), vm((512, 128), jnp.int32),
        vm((1, 512), jnp.int32), vm((CAP, 128), F32), vm((D, FF), BF), vm((D, FF), BF), vm((FF, D), BF),
        vm((TOK, D), BF), vm((TOK, D), BF), vm((TOK, D), BF),
        vm((TOK, D), F32), vm((2 * TOK, D), BF), vm((1024, 256), BF), vm((DEV, 16, 1024), BF),
        vm((DEV, 16, 1024), BF), vm((512, D), F32), vm((CAP, D), BF), vm((CAP, D), BF),
        vm((CAP, FF), BF), vm((CAP, FF), BF), vm((CAP, FF), BF), vm((512, 1024), BF),
        vm((DEV, 16, 512), BF), vm((DEV, 16, 512), BF),
        vm((TOK, D), F32), vm((TOK, D), BF),
    ] + [vm(state, BF)] * 8 + [
        vm((5, 1, D), F32), vm((4, 3, 1, D), F32), vm((CAP, 128), F32),
    ]
    dma = pltpu.SemaphoreType.DMA
    sems = [
        dma((13,)), dma((10,)), dma, dma((4,)), dma, dma((4,)), dma((4,)), dma((4,)), dma((4, 3)), dma((4, 3)),
        pltpu.SemaphoreType.REGULAR,
    ]
    return pl.pallas_call(
        mega,
        out_shape=[jax.ShapeDtypeStruct(a, b) for a, b in results],
        in_specs=[pl.BlockSpec(memory_space=pl.ANY)] * 13,
        out_specs=[pl.BlockSpec(memory_space=pl.ANY)] * len(results),
        scratch_shapes=scratch + sems,
        compiler_params=pltpu.CompilerParams(
            collective_id=0, has_side_effects=True, vmem_limit_bytes=63 * 1024 * 1024
        ),
        name="mega",
    )(*operands)


def attend(scale, q_ref, k_ref, v_ref, g_ref, prior_ref, later_ref, gq_ref, gk_ref, gv_ref):
    q, k, v, g = q_ref[...], k_ref[...], v_ref[...], g_ref[...]
    prior = prior_ref[...].reshape(HEAD, HEAD)
    later = later_ref[...].reshape(HEAD, HEAD)
    row = lax.broadcasted_iota(jnp.int32, (TOK, TOK), 0)
    col = lax.broadcasted_iota(jnp.int32, (TOK, TOK), 1)
    mix_a = jnp.where(row >= col, dot_nt(g, v), 0.0).astype(BF)
    mix_b = jnp.where(row >= col, dot_nt(q, k), 0.0).astype(BF)
    gq_ref[...] = (scale * (dot(mix_a, k) + dot_nt(g, prior))).astype(BF)
    gk_ref[...] = (scale * (dot_tn(mix_a, q) + dot_nt(v, later))).astype(BF)
    gv_ref[...] = (scale * (dot_tn(mix_b, g) + dot(k, later))).astype(BF)


def call_attend(scale, q, k, v, g, prior, later):
    tok = pl.BlockSpec((TOK, HEAD), lambda h: (0, h))
    st = pl.BlockSpec((2, 64, HEAD), lambda h: (h, 0, 0))
    return pl.pallas_call(
        functools.partial(attend, scale),
        grid=(HEADS,),
        out_shape=[jax.ShapeDtypeStruct((TOK, D), BF)] * 3,
        in_specs=[tok] * 4 + [st] * 2,
        out_specs=[tok] * 3,
        name="attend",
    )(q, k, v, g, prior, later)


def body(stream, cotangent, norm_gain, queries, key_vectors, value_vectors, expert_index, router_gates,
         gate_proj, up_proj, down_proj):
    z = lax.axis_index("grp")
    s = lax.axis_index("seq")
    here = z * PLANE + s
    local = expert_index - here * TOK
    t = jnp.arange(TOK)
    same = jnp.sum((local[:, None, :] == t[None, :, None]).astype(jnp.int32), axis=2)
    under = jnp.sum(
        ((local[:, None, :] >= 0) & (local[:, None, :] < t[None, :, None])).astype(jnp.int32), axis=2
    )
    code = (same * (under + 1)).astype(BF)
    own = lax.dynamic_index_in_dim(expert_index, here, 0, keepdims=False)
    src = own // TOK
    slot = jnp.sum((src[None, :] == src[:, None]) & (own[None, :] < own[:, None]), axis=1).astype(jnp.int32)
    x, y, c = s // 8, (s // 2) % 4, s % 2
    dz = (z - src // 32) % 4
    dx = (x - (src // 8) % 4) % 4
    dy = (y - (src // 2) % 4) % 4
    dc = (c - src % 2) % 2
    at = ((dz * 32 + dx * 8 + dy * 2 + dc) * MULT_INV) % DEV
    target = at * 8 + slot
    target = jnp.concatenate([target, target + 4])
    tcol = jnp.broadcast_to(target[:, None], (512, 128))
    trow = target[None, :]
    gates = jnp.broadcast_to(router_gates[0][:, None], (CAP, 128))
    rows, gout, hid, dgp, dup, router, g, prior, later, gain = call_mega(
        (stream, cotangent, norm_gain[None, :], code, tcol, trow, gates, gate_proj[0], up_proj[0], down_proj[0],
         queries, key_vectors, value_vectors)
    )
    scale = 1.0 / math.sqrt(HEAD * TOK * PLANE)
    gq, gk, gv = call_attend(scale, queries, key_vectors, value_vectors, g, prior, later)
    grad_down = dot_tn(hid, gout).astype(BF)
    grad_gate = dot_tn(rows, dgp).astype(BF)
    grad_up = dot_tn(rows, dup).astype(BF)
    return (g, gq, gk, gv, grad_gate[None], grad_up[None], grad_down[None], router[:, 0][None], gain[0])


def solution(mesh):
    both = ("grp", "seq")
    r2, r3 = P(both, None), P(both, None, None)
    return jax.shard_map(
        body,
        mesh=mesh,
        in_specs=(r2, r2, P(), r2, r2, r2, P(), r2, r3, r3, r3),
        out_specs=(r2, r2, r2, r2, r3, r3, r3, r2, P()),
        check_vma=False,
    )
```

time: 319 us -> 158 us (0.50)
  Pallas kernels: 0 us -> 135 us
  waiting for transfers between devices: 102 us -> 0 us
  local copies, waits for them, and re-layouts: 52.3 us -> 4.37 us
  other arithmetic: 54.8 us -> 7.07 us
  matrix products: 43.1 us -> 9.54 us
  blocking collectives: 29.4 us -> 0 us
  starting transfers between devices: 19.3 us -> 0 us
  between operations: 14.3 us -> 0.76 us
    pallas_call x0 -> x2, Pallas kernels: none -> 135 us  [the longest x1 124 us: call_mega(): pl.pallas_call(mega, out_shape=[jax.ShapeDtypeStruct(a, b) for a, b in re...]
    all_to_all x2 -> x0, waiting for transfers between devices: 68.8 us -> none  [the longest x1 34.5 us: body(): lax.all_to_all(back_rows.reshape(dev_count, most, width), GRP_SEQ, split_...]
    add x31 -> x1, other arithmetic: 39.8 us -> 0.05 us  [body(): target = jnp.concatenate([target, target + 4])]
    all_gather x4 -> x0, waiting for transfers between devices: 33.6 us -> none  [the longest x1 20.7 us: prefix(): gathered = lax.all_gather(shard.astype(jnp.bfloat16), axis)]
    dot_general x19 -> x3, matrix products: 43.1 us -> 9.54 us  [dot_tn(): lax.dot_general(a, b, (((0,), (0,)), ((), ())), preferred_element_type=F32)]
    gather x6 -> x0, local copies, waits for them, and re-layouts: 33.1 us -> none  [the longest x4 20.9 us: body(): outgoing = jnp.concatenate([inputs[picked], cotangent[picked]], axis=1)]
    psum x4 -> x0, blocking collectives: 29.4 us -> none  [one_axis_at_a_time(): shard = lax.psum(shard, axis)]
    all_to_all x2 -> x0, starting transfers between devices: 18.9 us -> none  [the longest x1 11.7 us: body(): lax.all_to_all(outgoing, GRP_SEQ, split_axis=0, concat_axis=0, tiled=True)]
  transfers between devices with their start and end apart: 6 -> 0, of which waited for: 4 -> 0; matrix products, arithmetic and copies ran while one was open for 20% -> 0% of each run, Pallas kernels for 0% -> 0%
where the time goes in v1:
time: 158 us; the launch traced here: 157 us
  Pallas kernels  135 us (85%)
  matrix products  9.54 us (6%)
  other arithmetic  7.07 us (4%)
  local copies, waits for them, and re-layouts  4.37 us (3%)
    pallas_call x1, Pallas kernels, call_mega(): pl.pallas_call(mega, out_shape=[jax.ShapeDtypeStruct(a, b) for a, b in re...  124 us
    pallas_call x1, Pallas kernels, call_attend(): pl.pallas_call(functools.partial(attend, scale), grid=(HEADS,), out_shape...  11.2 us
    dot_general x3, matrix products, dot_tn(): lax.dot_general(a, b, (((0,), (0,)), ((), ())), preferred_element_type=F32)  9.54 us
    reduce_sum x1, other arithmetic, body(): jnp.sum(((local[:, None, :] >= 0) & (local[:, None, :] < t[None, :, None]...  4.52 us

profile of v1, /device:TPU:0, one launch (start us, length us, event | category | flops | bytes accessed | tf_op | source)
XLA Modules:
  0.0 156.6 jit_solution(3762107809866228372)
XLA Ops:
  0.7 0.7 and_select_fusion
  1.4 0.2 convert_reduce_fusion.2
  1.7 0.0 copy-start.2
  1.7 0.8 broadcast_in_dim.17.tcol_h
  2.5 0.9 broadcast_compare_fusion
  3.5 4.5 %convert_reduce_fusion = (s32[128,128]{1,0:T(8,128)S(1)}, s32[128,128]{1,0:T(8,128)S(1)}) fusion(s32[128,256]{1,0:T(8,128)S(1)} %get-tuple-element.42, pred[128,256]{1,0:T(8,128)(4,1)S(1)} %get-tuple-element.41), kind=kLoop, calls=%fused_computation | loop fusion | flops 29327360 | bytes 294912 | tf_op jit(solution)/shard_map/reduce_sum | solution.py:438
  8.0 0.6 multiply_convert_fusion.code_h
  8.6 1.4 broadcast_in_dim.20.gates_h
  10.1 0.0 copy-done.2
  10.1 123.7 %mega.1 = (bf16[256,2048]{1,0:T(8,128)(2,1)}, bf16[256,2048]{1,0:T(8,128)(2,1)}, bf16[256,768]{1,0:T(8,128)(2,1)}, bf16[256,768]{1,0:T(8,128)(2,1)}, bf16[256,76...) custom-call(bf16[128,2048]{1,0:T(8,128)(2,1)} %stream_h.1, ...), custom_call_target="tpu_custom_call" | custom-call | tf_op jit(solution)/shard_map/mega/pallas_call | solution.py:391
  133.8 0.0 copy-start.4
  133.8 0.0 copy-start.6
  133.8 4.1 %fusion.3 = bf16[1,768,2048]{2,1,0:T(8,128)(2,1)} fusion(bf16[256,768]{1,0:T(8,128)(2,1)} %get-tuple-element.31, bf16[256,2048]{1,0:T(8,128)(2,1)} %get-tuple-element.32), kind=kOutput, calls=%fused_computation.10 | convolution fusion | flops 806879232 | bytes 4587520 | tf_op jit(solution)/shard_map/dot_general | solution.py:38
  137.9 0.0 copy-start.5
  137.9 0.0 copy-done.4
  137.9 0.0 copy-done.6
  137.9 2.7 %fusion.2 = bf16[1,2048,768]{2,1,0:T(8,128)(2,1)} fusion(bf16[256,2048]{1,0:T(8,128)(2,1)S(1)} %copy-done.4, bf16[256,768]{1,0:T(8,128)(2,1)S(1)} %copy-done.6), kind=kOutput, calls=%fused_computation.9 | convolution fusion | flops 806879232 | bytes 4587520 | tf_op jit(solution)/shard_map/dot_general | solution.py:38
  140.6 0.0 copy-done.5
  140.6 0.0 copy-start.1
  140.6 0.0 copy-start
  140.6 2.7 %fusion.1 = bf16[1,2048,768]{2,1,0:T(8,128)(2,1)} fusion(bf16[256,2048]{1,0:T(8,128)(2,1)S(1)} %copy-done.4, bf16[256,768]{1,0:T(8,128)(2,1)S(1)} %copy-done.5), kind=kOutput, calls=%fused_computation.8 | convolution fusion | flops 806879232 | bytes 4587520 | tf_op jit(solution)/shard_map/dot_general | solution.py:38
  143.3 0.0 copy-start.3
  143.3 11.2 %attend.1 = (bf16[128,2048]{1,0:T(8,128)(2,1)}, bf16[128,2048]{1,0:T(8,128)(2,1)}, bf16[128,2048]{1,0:T(8,128)(2,1)}) custom-call(bf16[128,2048]{1,0:T(8,128)(2,1)} %q_ref.1, bf16[128,2048]{1,0:T(8,128)(2,1)} %k_ref.1, bf16[128,2048]{1,0:T(8,128)(2,1)} %v_ref.1, bf16[128,2048]{1,0:T(8,128)(2,1)} %get-tuple-element.52.g_ref, ...), custom_call_target="tpu_custom_call" | custom-call | tf_op jit(solution)/shard_map/attend/pallas_call | solution.py:420
  154.5 0.0 copy-done.1
  154.5 0.7 slice_reduce_fusion
  155.2 0.0 copy-done
  155.2 0.8 copy.22
  156.0 0.0 copy-done.3
  156.0 0.6 copy.23
  (3 shorter events, 0.1 us)
Async XLA Ops:
  1.7 8.4 %copy-start.2 = (s32[512]{0:T(512)}, s32[512]{0:T(512)S(1)}, u32[]{:S(2)}) copy-start(s32[512]{0:T(512)S(1)} %pad_add_fusion) | copy-start | bytes 6148
  133.8 4.2 %copy-start.4 = (bf16[256,2048]{1,0:T(8,128)(2,1)S(1)}, bf16[256,2048]{1,0:T(8,128)(2,1)}, u32[]{:S(2)}) copy-start(bf16[256,2048]{1,0:T(8,128)(2,1)} %get-tuple-element.28) | copy-start | bytes 3145732
  133.8 4.1 %copy-start.6 = (bf16[256,768]{1,0:T(8,128)(2,1)S(1)}, bf16[256,768]{1,0:T(8,128)(2,1)}, u32[]{:S(2)}) copy-start(bf16[256,768]{1,0:T(8,128)(2,1)} %get-tuple-element.30) | copy-start | bytes 1179652
  137.9 2.7 %copy-start.5 = (bf16[256,768]{1,0:T(8,128)(2,1)S(1)}, bf16[256,768]{1,0:T(8,128)(2,1)}, u32[]{:S(2)}) copy-start(bf16[256,768]{1,0:T(8,128)(2,1)} %get-tuple-element.29) | copy-start | bytes 1179652
  140.6 13.9 %copy-start.1 = (f32[256,128]{1,0:T(8,128)S(1)}, f32[256,128]{1,0:T(8,128)}, u32[]{:S(2)}) copy-start(f32[256,128]{1,0:T(8,128)} %get-tuple-element.33) | copy-start | bytes 393220
  140.6 14.6 %copy-start = (bf16[128,2048]{1,0:T(8,128)(2,1)S(1)}, bf16[128,2048]{1,0:T(8,128)(2,1)}, u32[]{:S(2)}) copy-start(bf16[128,2048]{1,0:T(8,128)(2,1)} %get-tuple-element.52.g_ref) | copy-start | bytes 1572868
  143.3 12.7 %copy-start.3 = (f32[1,2048]{1,0:T(1,128)S(1)}, f32[1,2048]{1,0:T(1,128)}, u32[]{:S(2)}) copy-start(f32[1,2048]{1,0:T(1,128)} %get-tuple-element.34) | copy-start | bytes 24580

commit v2 on v1

v2 whole, which is shorter than its diff:
```python
import functools
import math

import jax
import jax.numpy as jnp
from jax import lax
from jax.experimental import pallas as pl
from jax.experimental.pallas import tpu as pltpu
from jax.sharding import PartitionSpec as P

D = 2048
FF = 768
HEADS = 16
HEAD = 128
CAP = 256
TOK = 128
DEV = 128
PLANE = 32
SLOTS = 4
EPS = 1e-06
MULT = 37
MULT_INV = 45
PLANE_MULT = 13
MESH = pl.DeviceIdType.MESH
BF = jnp.bfloat16
F32 = jnp.float32


def dot(a, b):
    return lax.dot_general(a, b, (((1,), (0,)), ((), ())), preferred_element_type=F32)


def dot_nt(a, b):
    return lax.dot_general(a, b, (((1,), (1,)), ((), ())), preferred_element_type=F32)


def dot_tn(a, b):
    return lax.dot_general(a, b, (((0,), (0,)), ((), ())), preferred_element_type=F32)


def rem(a, n):
    return lax.rem(a, jnp.int32(n))


def div(a, n):
    return lax.div(a, jnp.int32(n))


def offsets(i):
    k = rem(i * MULT, DEV)
    return div(k, 32), rem(div(k, 8), 4), rem(div(k, 2), 4), rem(k, 2)


def index_of(z, x, y, c):
    return rem(z, 4), rem(x, 4) * 8 + rem(y, 4) * 2 + rem(c, 2)


def mega(
    scale,
    stream_h, cot_h, gain_h, index_h, gates_h, wg_h, wu_h, wd_h, q_h, k_h, v_h,
    rows_o, gout_o, hid_o, dpre_o, router_o, g_o, gq_o, gk_o, gv_o, gain_o,
    stream, cot, gain, index, gates, wg, wu, wd, qv, kv, vv,
    normed, xin, tindex, code, p8, send, recv, acc, rows, dy, gout, ghid, hid, dpre, rowst, hidt, stacked,
    wgt, wut, wdt, rsend, rrecv,
    gin, g, qt, skv, sqg, kv1, kvs, kv2, qg1, qgs, qg2, mixb, pk, pv, gq, gk, gv, gpart, gland, router,
    lsem, osem, fsem, frsem, bsem, brsem, asem, arsem, gsem, grsem, zsem,
):
    z = lax.axis_index("grp")
    s = lax.axis_index("seq")
    x, y, c = div(s, 8), rem(div(s, 2), 4), rem(s, 2)

    def dev(z2, s2):
        return {"grp": z2, "seq": s2}

    def out_to(i):
        dz, dx, dy, dc = offsets(i)
        return dev(*index_of(z + dz, x + dx, y + dy, c + dc))

    def back_to(i):
        dz, dx, dy, dc = offsets(i)
        return dev(*index_of(z + 4 - dz, x + 4 - dx, y + 4 - dy, c + dc))

    def plane_to(j):
        k = rem(j * PLANE_MULT, PLANE)
        return index_of(z, x + div(k, 8), y + rem(div(k, 2), 4), c + rem(k, 2))[1]

    bar = pltpu.get_barrier_semaphore()

    def greet(j, carry):
        pl.semaphore_signal(bar, inc=1, device_id=dev(z, plane_to(j)), device_id_type=MESH)
        return carry

    lax.fori_loop(1, PLANE, greet, 0)
    for d in (1, 2, 3):
        pl.semaphore_signal(bar, inc=1, device_id=dev(rem(z + d, 4), s), device_id_type=MESH)

    loads = [
        (index_h, index), (stream_h, stream), (cot_h, cot), (gain_h, gain),
        (gates_h, gates), (q_h, qv), (k_h, kv), (v_h, vv), (wg_h, wg), (wu_h, wu), (wd_h, wd),
    ]
    load = [pltpu.make_async_copy(a, b, lsem.at[n]) for n, (a, b) in enumerate(loads)]
    for cp in load:
        cp.start()

    load[0].wait()
    here = z * PLANE + s
    tindex[...] = (index[...] - here * TOK).astype(F32).T
    token = lax.broadcasted_iota(jnp.int32, (TOK, DEV), 0).astype(F32)

    def match(n, found):
        eight = tindex[pl.ds(pl.multiple_of(n * 8, 8), 8), :]
        for r in range(8):
            found = jnp.where(eight[r:r + 1, :] == token, 1.0, found)
        return found

    found = lax.fori_loop(0, CAP // 8, match, jnp.zeros((TOK, DEV), F32))
    earlier = lax.broadcasted_iota(jnp.int32, (TOK, TOK), 0) > lax.broadcasted_iota(jnp.int32, (TOK, TOK), 1)
    before = dot(jnp.where(earlier, 1.0, 0.0).astype(BF), found.astype(BF))
    code[...] = (found * (before + 1.0)).astype(BF)

    pl.semaphore_wait(bar, PLANE - 1 + 3)
    for d in (1, 2, 3):
        pl.semaphore_signal(zsem, inc=1, device_id=dev(rem(z + d, 4), s), device_id_type=MESH)

    def build(gi, carry):
        r = lax.broadcasted_iota(jnp.int32, (256, 128), 0) + gi * 256
        lane = lax.broadcasted_iota(jnp.int32, (256, 128), 1)
        k = ((r >> 3) * MULT) & (DEV - 1)
        e = ((z + (k >> 5)) & 3) * 32 + ((x + (k >> 3)) & 3) * 8 + ((y + (k >> 1)) & 3) * 2 + ((c + k) & 1)
        pick = jnp.where(e == lane, 1.0, 0.0).astype(BF)
        rep = dot_nt(pick, code[...])
        want = ((r & 3) + 1).astype(F32)
        hit = jnp.where(rep == want, 1.0, 0.0)
        half = (r >> 2) & 1
        row0 = pl.multiple_of(gi * 256, 256)
        p8[pl.ds(row0, 256), 0:128] = jnp.where(half == 0, hit, 0.0).astype(BF)
        p8[pl.ds(row0, 256), 128:256] = jnp.where(half == 1, hit, 0.0).astype(BF)
        return carry

    lax.fori_loop(0, 4, build, 0)

    def fold(o):
        o = o.reshape(32, 8, 1024)
        return jnp.concatenate([o[:, :, 0:512], o[:, :, 512:1024]], axis=1).astype(BF)

    def fill(kind):
        def one(gi, carry):
            row0 = pl.multiple_of(gi * 256, 256)
            send[kind, pl.ds(gi * 32, 32)] = fold(dot(p8[pl.ds(row0, 256), :], xin[kind]))
            return carry

        lax.fori_loop(0, 4, one, 0)

    def push(kind):
        def one(i, carry):
            pltpu.make_async_remote_copy(
                send.at[kind, i], recv.at[kind, i], fsem.at[kind], frsem.at[kind, div(i, 32)],
                device_id=out_to(i), device_id_type=MESH,
            ).start()
            return carry

        lax.fori_loop(1, DEV, one, 0)
        recv[kind, 0] = send[kind, 0]

    load[2].wait()
    xin[0, 0:TOK, :] = cot[:, 0:1024]
    xin[0, TOK:, :] = cot[:, 1024:]
    fill(0)
    pl.semaphore_wait(zsem, 3)
    push(0)

    load[1].wait()
    load[3].wait()
    wide = stream[...].astype(F32)
    inv = lax.rsqrt(jnp.mean(wide * wide, axis=1, keepdims=True) + EPS)
    nrm = wide * inv
    normed[...] = nrm
    xin[1, 0:TOK, :] = (nrm * gain[...])[:, 0:1024].astype(BF)
    xin[1, TOK:, :] = (nrm * gain[...])[:, 1024:].astype(BF)
    fill(1)
    push(1)

    for n in (4, 5, 6, 7):
        load[n].wait()
    tril = lax.broadcasted_iota(jnp.int32, (TOK, TOK), 0) >= lax.broadcasted_iota(jnp.int32, (TOK, TOK), 1)

    def head(h):
        return pl.ds(pl.multiple_of(h * HEAD, HEAD), HEAD)

    def local_kv(h, carry):
        kh = kv[:, head(h)]
        skv[pl.ds(2 * h, 2)] = dot_tn(kh, vv[:, head(h)]).reshape(2, 64, HEAD).astype(BF)
        qt[head(h), :] = qv[:, head(h)].T
        mixb[h] = jnp.where(tril, dot_nt(qv[:, head(h)], kh), 0.0).astype(BF)
        return carry

    lax.fori_loop(0, HEADS, local_kv, 0)

    def scatter(src, dst, sem, rsem):
        def one(j, carry):
            to = plane_to(j)
            pltpu.make_async_remote_copy(
                src.at[to], dst.at[s], sem, rsem, device_id=dev(z, to), device_id_type=MESH
            ).start()
            return carry

        lax.fori_loop(1, PLANE, one, 0)
        dst[s] = src[s]

    def arrived(dst, rsem):
        span = dst.at[pl.ds(0, PLANE - 1)]
        pltpu.make_async_copy(span, span, rsem).wait()

    scatter(skv, kv1, asem.at[0], arsem.at[0])

    own_row = index[pl.ds(here, 1), :]
    own_col = jnp.broadcast_to(own_row.astype(F32), (8, CAP)).T[:, 0:1].astype(jnp.int32)
    wide_row = jnp.broadcast_to(own_row, (CAP, CAP))
    wide_col = jnp.broadcast_to(own_col, (CAP, CAP))
    mate = (wide_row >> 7) == (wide_col >> 7)
    slot_col = jnp.sum(jnp.where(mate & (wide_row < wide_col), 1.0, 0.0), axis=1, keepdims=True)
    slot_row = jnp.sum(jnp.where(mate & (wide_col < wide_row), 1.0, 0.0), axis=0, keepdims=True)

    def place(own, slot):
        src = own >> 7
        k = (
            ((z - (src >> 5)) & 3) * 32 + ((x - (src >> 3)) & 3) * 8 + ((y - (src >> 1)) & 3) * 2 + ((c - src) & 1)
        )
        return ((k * MULT_INV) & (DEV - 1)) * 8 + slot.astype(jnp.int32)

    at_col = place(own_col, slot_col)
    at_row = place(own_row, slot_row)
    tcol = jnp.concatenate([at_col, at_col + 4], axis=0)
    trow = jnp.concatenate([at_row, at_row + 4], axis=1)
    gate_col = jnp.broadcast_to(gates[...], (8, CAP)).T[:, 0:1]

    for n in (8, 9, 10):
        load[n].wait()

    def turn_weights(n, carry):
        c0 = pl.multiple_of(n * 256, 256)
        wgt[:, pl.ds(c0, 256)] = wg[pl.ds(c0, 256), :].T
        wut[:, pl.ds(c0, 256)] = wu[pl.ds(c0, 256), :].T
        wdt[pl.ds(c0, 256), :] = wd[:, pl.ds(c0, 256)].T
        return carry

    lax.fori_loop(0, 8, turn_weights, 0)

    def settle(kind, dst):
        for gi in range(4):
            first = 1 if gi == 0 else 0
            span = recv.at[kind, pl.ds(gi * 32 + first, 32 - first)]
            pltpu.make_async_copy(span, span, frsem.at[kind, gi]).wait()
            lane = lax.broadcasted_iota(jnp.int32, (512, 256), 1) + gi * 256
            put = jnp.where(lane == tcol, 1.0, 0.0).astype(BF)
            for half in range(2):
                f = recv[kind, pl.ds(gi * 32, 32)].astype(F32).reshape(32, 2, 8, 512)[:, half]
                part = dot(put, f.reshape(256, 512).astype(BF))
                at = slice(half * 512, (half + 1) * 512)
                if gi == 0:
                    acc[:, at] = part
                elif gi < 3:
                    acc[:, at] += part
                else:
                    part = (acc[:, at] + part).astype(BF)
                    dst[:, half * 512:(half + 1) * 512] = part[0:CAP]
                    dst[:, 1024 + half * 512:1024 + (half + 1) * 512] = part[CAP:]

    settle(0, dy)
    gout[...] = (gate_col * dy[...].astype(F32)).astype(BF)
    ghid[...] = dot(gout[...], wdt[...])
    settle(1, rows)

    def front(n, carry):
        c0 = pl.multiple_of(n * 256, 256)
        gp = dot(rows[...], wg[:, pl.ds(c0, 256)])
        up = dot(rows[...], wu[:, pl.ds(c0, 256)])
        gh = ghid[:, pl.ds(c0, 256)]
        sg = jax.nn.sigmoid(gp)
        silu = gp * sg
        hid[:, pl.ds(c0, 256)] = (silu * up).astype(BF)
        dpre[:, pl.ds(c0, 256)] = (gh * up * (sg * (1.0 + gp * (1.0 - sg)))).astype(BF)
        dpre[:, pl.ds(pl.multiple_of(c0 + FF, 256), 256)] = (gh * silu).astype(BF)
        return carry

    lax.fori_loop(0, 3, front, 0)

    def back(n, carry):
        r0 = pl.multiple_of(n * 256, 256)
        gr = dot(dpre[:, 0:FF], wgt[:, pl.ds(r0, 256)]) + dot(dpre[:, FF:], wut[:, pl.ds(r0, 256)])
        h0 = pl.multiple_of(div(n, 4) * 256, 256)
        c0 = pl.multiple_of(rem(n, 4) * 256, 256)
        stacked[pl.ds(h0, 256), pl.ds(c0, 256)] = gr.astype(BF)
        return carry

    lax.fori_loop(0, 8, back, 0)

    def refill(gi, carry):
        r = lax.broadcasted_iota(jnp.int32, (256, 512), 0) + gi * 256
        put = jnp.where(r == trow, 1.0, 0.0).astype(BF)
        rsend[pl.ds(gi * 32, 32)] = fold(dot(put, stacked[...]))
        return carry

    def ret(i, carry):
        pltpu.make_async_remote_copy(
            rsend.at[i], rrecv.at[i], bsem, brsem.at[div(i, 32)], device_id=back_to(i), device_id_type=MESH
        ).start()
        return carry

    lax.fori_loop(0, 2, refill, 0)
    lax.fori_loop(1, 32, ret, 0)
    lax.fori_loop(2, 3, refill, 0)
    lax.fori_loop(32, 64, ret, 0)
    lax.fori_loop(3, 4, refill, 0)
    lax.fori_loop(64, 128, ret, 0)
    rrecv[0] = rsend[0]

    def turn(n, carry):
        c0 = pl.multiple_of(n * 256, 256)
        rowst[pl.ds(c0, 256), :] = rows[:, pl.ds(c0, 256)].T
        return carry

    lax.fori_loop(0, 8, turn, 0)
    for n in range(3):
        hidt[n * 256:(n + 1) * 256, :] = hid[:, n * 256:(n + 1) * 256].T
    outs = [(rowst, rows_o), (gout, gout_o), (hidt, hid_o), (dpre, dpre_o)]
    store = [pltpu.make_async_copy(a, b, osem.at[n]) for n, (a, b) in enumerate(outs)]
    for cp in store:
        cp.start()

    def route(n, total):
        c0 = pl.multiple_of(n * 256, 256)
        eo = dot(hid[...], wd[:, pl.ds(c0, 256)])
        return total + jnp.sum(dy[:, pl.ds(c0, 256)].astype(F32) * eo, axis=1, keepdims=True)

    router_col = lax.fori_loop(0, 8, route, jnp.zeros((CAP, 1), F32))
    router[...] = jnp.broadcast_to(router_col, (CAP, 128)).T[0:1, :]

    arrived(kv1, arsem.at[0])

    def prefix(r, total):
        kvs[r] = total.astype(BF)
        return total + kv1[r].astype(F32)

    lax.fori_loop(0, PLANE, prefix, jnp.zeros((64, HEAD), F32))
    scatter(kvs, kv2, asem.at[1], arsem.at[1])

    for gi in range(4):
        first = 1 if gi == 0 else 0
        span = rrecv.at[pl.ds(gi * 32 + first, 32 - first)]
        pltpu.make_async_copy(span, span, brsem.at[gi]).wait()
        for half in range(2):
            f = rrecv[pl.ds(gi * 32, 32)].astype(F32).reshape(32, 2, 8, 512)[:, half]
            f = f.reshape(256, 512).astype(BF)
            part = dot_tn(p8[gi * 256:(gi + 1) * 256, :], f)
            for hh in range(2):
                c0 = hh * 1024 + half * 512
                piece = part[hh * TOK:(hh + 1) * TOK, :]
                if gi == 0:
                    gin[:, c0:c0 + 512] = piece
                else:
                    gin[:, c0:c0 + 512] += piece

    gi_ = gin[...]
    nrm = normed[...]

    def spread(stage):
        if stage == 0:
            to = [dev(z, s + 1 - 2 * c)]
        elif stage == 1:
            to = [dev(z, x * 8 + rem(y + d, 4) * 2 + c) for d in (1, 2, 3)]
        elif stage == 2:
            to = [dev(z, rem(x + d, 4) * 8 + y * 2 + c) for d in (1, 2, 3)]
        else:
            to = [dev(rem(z + d, 4), s) for d in (1, 2, 3)]
        cps = [
            pltpu.make_async_remote_copy(
                gpart.at[stage], gland.at[stage, d], gsem.at[stage, d], grsem.at[stage, d],
                device_id=t, device_id_type=MESH,
            )
            for d, t in enumerate(to)
        ]
        for cp in cps:
            cp.start()
        return cps

    def collect(stage, cps):
        for cp in cps:
            cp.wait()
        total = gpart[stage]
        for d in range(len(cps)):
            total = total + gland[stage, d]
        return total

    gpart[0] = jnp.sum(gi_ * nrm, axis=0, keepdims=True)
    cps0 = spread(0)

    gn = gi_ * gain[...]
    wide_g = cot[...].astype(F32) + inv * (gn - nrm * jnp.mean(gn * nrm, axis=1, keepdims=True))
    g[...] = wide_g.astype(BF)
    gcp = pltpu.make_async_copy(g, g_o, osem.at[4])
    gcp.start()
    for h in range(HEADS):
        at = slice(h * HEAD, (h + 1) * HEAD)
        sqg[2 * h:2 * h + 2] = dot(qt[at, :], g[:, at]).reshape(2, 64, HEAD).astype(BF)
    scatter(sqg, qg1, asem.at[2], arsem.at[2])
    gpart[1] = collect(0, cps0)
    cps1 = spread(1)

    def local_terms(h, carry):
        gh = g[:, head(h)]
        mix_a = jnp.where(tril, dot_nt(gh, vv[:, head(h)]), 0.0).astype(BF)
        gin[:, head(h)] = dot(mix_a, kv[:, head(h)])
        pk[:, head(h)] = dot_tn(mix_a, qv[:, head(h)])
        pv[:, head(h)] = dot_tn(mixb[h], gh)
        return carry

    lax.fori_loop(0, HEADS, local_terms, 0)
    arrived(qg1, arsem.at[2])

    def suffix(n, total):
        r = PLANE - 1 - n
        qgs[r] = total.astype(BF)
        return total + qg1[r].astype(F32)

    lax.fori_loop(0, PLANE, suffix, jnp.zeros((64, HEAD), F32))
    scatter(qgs, qg2, asem.at[3], arsem.at[3])
    gpart[2] = collect(1, cps1)
    cps2 = spread(2)
    arrived(kv2, arsem.at[1])

    def early_terms(h, carry):
        prior = kv2[pl.ds(2 * h, 2)].reshape(HEAD, HEAD)
        gq[:, head(h)] = (scale * (gin[:, head(h)] + dot_nt(g[:, head(h)], prior))).astype(BF)
        return carry

    lax.fori_loop(0, HEADS, early_terms, 0)
    late = [pltpu.make_async_copy(gq, gq_o, osem.at[5])]
    late[0].start()
    gpart[3] = collect(2, cps2)
    cps3 = spread(3)
    arrived(qg2, arsem.at[3])
    for h in range(HEADS):
        at = slice(h * HEAD, (h + 1) * HEAD)
        later = qg2[2 * h:2 * h + 2].reshape(HEAD, HEAD)
        gk[:, at] = (scale * (pk[:, at] + dot_nt(vv[:, at], later))).astype(BF)
        gv[:, at] = (scale * (pv[:, at] + dot(kv[:, at], later))).astype(BF)
    gpart[4] = collect(3, cps3)
    for n, (a, b) in enumerate([(gk, gk_o), (gv, gv_o), (gpart.at[4], gain_o), (router, router_o)]):
        late.append(pltpu.make_async_copy(a, b, osem.at[6 + n]))
        late[-1].start()

    for kind in (0, 1):
        span = send.at[kind, pl.ds(1, DEV - 1)]
        pltpu.make_async_copy(span, span, fsem.at[kind]).wait()
    span = rsend.at[pl.ds(1, DEV - 1)]
    pltpu.make_async_copy(span, span, bsem).wait()
    for n, buf in enumerate((skv, kvs, sqg, qgs)):
        arrived(buf, asem.at[n])
    for cp in store + [gcp] + late:
        cp.wait()


def call_mega(scale, operands):
    def vm(shape, dtype):
        return pltpu.VMEM(shape, dtype)

    state = (PLANE, 64, HEAD)
    results = [
        ((D, CAP), BF), ((CAP, D), BF), ((FF, CAP), BF), ((CAP, 2 * FF), BF), ((1, CAP), F32),
        ((TOK, D), BF), ((TOK, D), BF), ((TOK, D), BF), ((TOK, D), BF), ((1, D), F32),
    ]
    scratch = [
        vm((TOK, D), BF), vm((TOK, D), BF), vm((1, D), F32), vm((DEV, CAP), jnp.int32), vm((1, CAP), F32),
        vm((D, FF), BF), vm((D, FF), BF), vm((FF, D), BF),
        vm((TOK, D), BF), vm((TOK, D), BF), vm((TOK, D), BF),
        vm((TOK, D), F32), vm((2, 256, 1024), BF), vm((CAP, DEV), F32), vm((TOK, DEV), BF), vm((1024, 256), BF),
        vm((2, DEV, 16, 512), BF), vm((2, DEV, 16, 512), BF), vm((512, 1024), F32), vm((CAP, D), BF),
        vm((CAP, D), BF), vm((CAP, D), BF), vm((CAP, FF), F32), vm((CAP, FF), BF), vm((CAP, 2 * FF), BF),
        vm((D, CAP), BF), vm((FF, CAP), BF), vm((512, 1024), BF),
        vm((FF, D), BF), vm((FF, D), BF), vm((D, FF), BF),
        vm((DEV, 16, 512), BF), vm((DEV, 16, 512), BF),
        vm((TOK, D), F32), vm((TOK, D), BF),
        vm((D, TOK), BF),
    ] + [vm(state, BF)] * 8 + [
        vm((HEADS, HEAD, HEAD), BF), vm((TOK, D), F32), vm((TOK, D), F32),
        vm((TOK, D), BF), vm((TOK, D), BF), vm((TOK, D), BF),
        vm((5, 1, D), F32), vm((4, 3, 1, D), F32), vm((1, CAP), F32),
    ]
    dma = pltpu.SemaphoreType.DMA
    sems = [
        dma((11,)), dma((10,)), dma((2,)), dma((2, 4)), dma, dma((4,)), dma((4,)), dma((4,)), dma((4, 3)), dma((4, 3)),
        pltpu.SemaphoreType.REGULAR,
    ]
    return pl.pallas_call(
        functools.partial(mega, scale),
        out_shape=[jax.ShapeDtypeStruct(a, b) for a, b in results],
        in_specs=[pl.BlockSpec(memory_space=pl.ANY)] * 11,
        out_specs=[pl.BlockSpec(memory_space=pl.ANY)] * len(results),
        scratch_shapes=scratch + sems,
        compiler_params=pltpu.CompilerParams(
            collective_id=0, has_side_effects=True, vmem_limit_bytes=63 * 1024 * 1024
        ),
        name="mega",
    )(*operands)


def finish(
    rowst_h, gout_h, hidt_h, dpre_h, router_h, g_h, gq_h, gk_h, gv_h, gain_h,
    gate_o, up_o, down_o, router_o, g_o, gq_o, gk_o, gv_o, gain_o,
    rowst, gout, hidt, dpre, router, g, gq, gk, gv, gain, gate, up, down, lsem, psem, wsem,
):
    ins = [(hidt_h, hidt), (gout_h, gout), (rowst_h, rowst), (dpre_h, dpre)]
    loads = [pltpu.make_async_copy(a, b, lsem.at[n]) for n, (a, b) in enumerate(ins)]
    through = [(g_h, g, g_o), (gq_h, gq, gq_o), (gk_h, gk, gk_o), (gv_h, gv, gv_o), (router_h, router, router_o),
               (gain_h, gain, gain_o)]
    take = [pltpu.make_async_copy(a, b, lsem.at[4 + n]) for n, (a, b, o) in enumerate(through)]
    give = [pltpu.make_async_copy(b, o, psem.at[n]) for n, (a, b, o) in enumerate(through)]
    for cp in loads + take:
        cp.start()
    writes = []

    def put(src, dst, rows):
        cp = pltpu.make_async_copy(src.at[rows], dst.at[rows], wsem.at[len(writes)])
        cp.start()
        writes.append(cp)

    loads[0].wait()
    loads[1].wait()
    for n in range(3):
        r = pl.ds(n * 256, 256)
        for m in range(2):
            col = pl.ds(m * 1024, 1024)
            down[r, col] = dot(hidt[r, :], gout[:, col]).astype(BF)
        put(down, down_o, r)
    loads[2].wait()
    loads[3].wait()
    for n in range(8):
        r = pl.ds(n * 256, 256)
        gate[r, :] = dot(rowst[r, :], dpre[:, 0:FF]).astype(BF)
        put(gate, gate_o, r)
        up[r, :] = dot(rowst[r, :], dpre[:, FF:]).astype(BF)
        put(up, up_o, r)
        if n < len(through):
            take[n].wait()
            give[n].start()
    for cp in give + writes:
        cp.wait()


def call_finish(operands):
    def vm(shape, dtype):
        return pltpu.VMEM(shape, dtype)

    small = [((1, CAP), F32), ((TOK, D), BF), ((TOK, D), BF), ((TOK, D), BF), ((TOK, D), BF), ((1, D), F32)]
    weights = [((D, FF), BF), ((D, FF), BF), ((FF, D), BF)]
    dma = pltpu.SemaphoreType.DMA
    return pl.pallas_call(
        finish,
        out_shape=[jax.ShapeDtypeStruct(a, b) for a, b in weights + small],
        in_specs=[pl.BlockSpec(memory_space=pl.ANY)] * 10,
        out_specs=[pl.BlockSpec(memory_space=pl.ANY)] * 9,
        scratch_shapes=[vm((D, CAP), BF), vm((CAP, D), BF), vm((FF, CAP), BF), vm((CAP, 2 * FF), BF)]
        + [vm(a, b) for a, b in small + weights]
        + [dma((10,)), dma((6,)), dma((19,))],
        compiler_params=pltpu.CompilerParams(vmem_limit_bytes=63 * 1024 * 1024),
        name="finish",
    )(*operands)


def body(stream, cotangent, norm_gain, queries, key_vectors, value_vectors, expert_index, router_gates,
         gate_proj, up_proj, down_proj):
    scale = 1.0 / math.sqrt(HEAD * TOK * PLANE)
    results = call_mega(scale, (
        stream, cotangent, norm_gain[None, :], expert_index, router_gates, gate_proj[0], up_proj[0], down_proj[0],
        queries, key_vectors, value_vectors,
    ))
    gate, up, down, router, g, gq, gk, gv, gain = call_finish(results)
    return (g, gq, gk, gv, gate[None], up[None], down[None], router, gain[0])


def solution(mesh):
    both = ("grp", "seq")
    r2, r3 = P(both, None), P(both, None, None)
    return jax.shard_map(
        body,
        mesh=mesh,
        in_specs=(r2, r2, P(), r2, r2, r2, P(), r2, r3, r3, r3),
        out_specs=(r2, r2, r2, r2, r3, r3, r3, r2, P()),
        check_vma=False,
    )
```

time: 158 us -> 126 us (0.80); the launches traced: 157 us -> 126 us
  Pallas kernels: 135 us -> 125 us
  matrix products: 9.54 us -> 0 us
  other arithmetic: 7.07 us -> 0 us
  local copies, waits for them, and re-layouts: 4.37 us -> 0 us
    dot_general x3 -> x0, matrix products: 9.54 us -> none  [dot_tn(): lax.dot_general(a, b, (((0,), (0,)), ((), ())), preferred_element_type=F32)]
    pallas_call x2, Pallas kernels: 135 us -> 125 us  [the longest x1 119 us: call_mega(): pl.pallas_call(functools.partial(mega, scale), out_shape=[jax.ShapeDtypeS...]
    reduce_sum x2 -> x0, other arithmetic: 4.73 us -> none  [the longest x1 4.52 us: body(): jnp.sum(((local[:, None, :] >= 0) & (local[:, None, :] < t[None, :, None]...]
    broadcast_in_dim x2 -> x0, local copies, waits for them, and re-layouts: 2.27 us -> none  [the longest x1 1.43 us: body(): gates = jnp.broadcast_to(router_gates[0][:, None], (CAP, 128))]
where the time goes in v2:
time: 126 us
  Pallas kernels  125 us (99%)
    pallas_call x1, Pallas kernels, call_mega(): pl.pallas_call(functools.partial(mega, scale), out_shape=[jax.ShapeDtypeS...  119 us
    pallas_call x1, Pallas kernels, call_finish(): pl.pallas_call(finish, out_shape=[jax.ShapeDtypeStruct(a, b) for a, b in...  6.33 us

profile of v2, /device:TPU:0, one launch (start us, length us, event | category | flops | bytes accessed | tf_op | source)
XLA Modules:
  0.0 126.3 jit_solution(17356468746079391986)
XLA Ops:
  0.6 119.2 %mega.1 = (bf16[2048,256]{1,0:T(8,128)(2,1)}, bf16[256,2048]{1,0:T(8,128)(2,1)}, bf16[768,256]{1,0:T(8,128)(2,1)}, bf16[256,1536]{1,0:T(8,128)(2,1)}, f32[1,256]...) custom-call(bf16[128,2048]{1,0:T(8,128)(2,1)} %stream_h.1, ...), custom_call_target="tpu_custom_call" | custom-call | tf_op jit(solution)/shard_map/mega/pallas_call | solution.py:495
  119.8 6.3 %finish.1 = (bf16[2048,768]{1,0:T(8,128)(2,1)}, bf16[2048,768]{1,0:T(8,128)(2,1)}, bf16[768,2048]{1,0:T(8,128)(2,1)}, f32[1,256]{1,0:T(1,128)}, bf16[128,2048]{1...) custom-call(bf16[2048,256]{1,0:T(8,128)(2,1)} %get-tuple-element.28., ...), custom_call_target="tpu_custom_call" | custom-call | tf_op jit(solution)/shard_map/finish/pallas_call | solution.py:558

commit v3 on v2

--- a/solution.py
+++ b/solution.py
@@ -16,10 +16,12 @@
 TOK = 128
 DEV = 128
 PLANE = 32
+CHIPS = 16
+CHIP_MULT = 7
 SLOTS = 4
 EPS = 1e-06
-MULT = 37
-MULT_INV = 45
+MULT = 91
+MULT_INV = 83
 PLANE_MULT = 13
 MESH = pl.DeviceIdType.MESH
 BF = jnp.bfloat16
@@ -62,8 +64,8 @@
     stream, cot, gain, index, gates, wg, wu, wd, qv, kv, vv,
     normed, xin, tindex, code, p8, send, recv, acc, rows, dy, gout, ghid, hid, dpre, rowst, hidt, stacked,
     wgt, wut, wdt, rsend, rrecv,
-    gin, g, qt, skv, sqg, kv1, kvs, kv2, qg1, qgs, qg2, mixb, pk, pv, gq, gk, gv, gpart, gland, router,
-    lsem, osem, fsem, frsem, bsem, brsem, asem, arsem, gsem, grsem, zsem,
+    gin, g, qt, skv, sqg, okv, oqg, kv2, qg2, tkv, kv1, kvs, tqg, qg1, qgs, mixb, pk, pv, gq, gk, gv, gpart, gland, router,
+    lsem, osem, fsem, frsem, bsem, brsem, asem, arsem, wsem, wrsem, gsem, grsem, zsem,
 ):
     z = lax.axis_index("grp")
     s = lax.axis_index("seq")
@@ -196,22 +198,39 @@
 
     lax.fori_loop(0, HEADS, local_kv, 0)
 
-    def scatter(src, dst, sem, rsem):
+    chip = x * 4 + y
+    mine = pl.ds(c * CHIPS, CHIPS)
+    theirs = pl.ds((1 - c) * CHIPS, CHIPS)
+
+    def swap(src, dst, part, n):
+        cp = pltpu.make_async_remote_copy(
+            src.at[part], dst.at[part], wsem.at[n], wrsem.at[n], device_id=dev(z, s + 1 - 2 * c), device_id_type=MESH
+        )
+        cp.start()
+        return cp
+
+    def landed(dst, part, n):
+        span = dst.at[part]
+        pltpu.make_async_copy(span, span, wrsem.at[n]).wait()
+
+    def scatter(src, dst, base, at, n):
         def one(j, carry):
-            to = plane_to(j)
+            k = rem(j * CHIP_MULT, CHIPS)
+            x2, y2 = rem(x + div(k, 4), 4), rem(y + rem(k, 4), 4)
             pltpu.make_async_remote_copy(
-                src.at[to], dst.at[s], sem, rsem, device_id=dev(z, to), device_id_type=MESH
+                src.at[x2 * 4 + y2], dst.at[base + at], asem.at[n], arsem.at[n],
+                device_id=dev(z, x2 * 8 + y2 * 2 + c), device_id_type=MESH,
             ).start()
             return carry
 
-        lax.fori_loop(1, PLANE, one, 0)
-        dst[s] = src[s]
-
-    def arrived(dst, rsem):
-        span = dst.at[pl.ds(0, PLANE - 1)]
-        pltpu.make_async_copy(span, span, rsem).wait()
-
-    scatter(skv, kv1, asem.at[0], arsem.at[0])
+        lax.fori_loop(1, CHIPS, one, 0)
+        dst[base + at] = src[at]
+
+    def arrived(dst, sem):
+        span = dst.at[pl.ds(0, CHIPS - 1)]
+        pltpu.make_async_copy(span, span, sem).wait()
+
+    swaps = [swap(skv, okv, theirs, 0), swap(skv, okv, mine, 1)]
 
     own_row = index[pl.ds(here, 1), :]
     own_col = jnp.broadcast_to(own_row.astype(F32), (8, CAP)).T[:, 0:1].astype(jnp.int32)
@@ -245,6 +264,9 @@
         return carry
 
     lax.fori_loop(0, 8, turn_weights, 0)
+    landed(okv, mine, 0)
+    tkv[...] = (skv[mine].astype(F32) + okv[mine].astype(F32)).astype(BF)
+    scatter(tkv, kv1, 0, chip, 0)
 
     def settle(kind, dst):
         for gi in range(4):
@@ -342,8 +364,8 @@
         kvs[r] = total.astype(BF)
         return total + kv1[r].astype(F32)
 
-    lax.fori_loop(0, PLANE, prefix, jnp.zeros((64, HEAD), F32))
-    scatter(kvs, kv2, asem.at[1], arsem.at[1])
+    lax.fori_loop(0, CHIPS, prefix, jnp.zeros((64, HEAD), F32))
+    scatter(kvs, kv2, c * CHIPS, chip, 1)
 
     for gi in range(4):
         first = 1 if gi == 0 else 0
@@ -400,10 +422,16 @@
     g[...] = wide_g.astype(BF)
     gcp = pltpu.make_async_copy(g, g_o, osem.at[4])
     gcp.start()
-    for h in range(HEADS):
-        at = slice(h * HEAD, (h + 1) * HEAD)
-        sqg[2 * h:2 * h + 2] = dot(qt[at, :], g[:, at]).reshape(2, 64, HEAD).astype(BF)
-    scatter(sqg, qg1, asem.at[2], arsem.at[2])
+    for part in range(2):
+        for n in range(8):
+            h = part * 8 + n + (8 - 16 * part) * (1 - c)
+            sqg[pl.ds(2 * h, 2)] = dot(qt[head(h), :], g[:, head(h)]).reshape(2, 64, HEAD).astype(BF)
+        swaps.append(swap(sqg, oqg, (theirs, mine)[part], 2 + part))
+    landed(oqg, mine, 2)
+    tqg[...] = (sqg[mine].astype(F32) + oqg[mine].astype(F32)).astype(BF)
+    scatter(tqg, qg1, 0, chip, 2)
+    arrived(kv2, arsem.at[1])
+    swaps.append(swap(kv2, kv2, mine, 4))
     gpart[1] = collect(0, cps0)
     cps1 = spread(1)
 
@@ -419,18 +447,21 @@
     arrived(qg1, arsem.at[2])
 
     def suffix(n, total):
-        r = PLANE - 1 - n
+        r = CHIPS - 1 - n
         qgs[r] = total.astype(BF)
         return total + qg1[r].astype(F32)
 
-    lax.fori_loop(0, PLANE, suffix, jnp.zeros((64, HEAD), F32))
-    scatter(qgs, qg2, asem.at[3], arsem.at[3])
+    lax.fori_loop(0, CHIPS, suffix, jnp.zeros((64, HEAD), F32))
+    scatter(qgs, qg2, c * CHIPS, chip, 3)
     gpart[2] = collect(1, cps1)
     cps2 = spread(2)
-    arrived(kv2, arsem.at[1])
+    landed(okv, theirs, 1)
+    landed(kv2, theirs, 4)
+    second = c.astype(F32)
 
     def early_terms(h, carry):
-        prior = kv2[pl.ds(2 * h, 2)].reshape(HEAD, HEAD)
+        two = pl.ds(2 * h, 2)
+        prior = (kv2[two].astype(F32) + second * okv[two].astype(F32)).reshape(HEAD, HEAD).astype(BF)
         gq[:, head(h)] = (scale * (gin[:, head(h)] + dot_nt(g[:, head(h)], prior))).astype(BF)
         return carry
 
@@ -440,9 +471,15 @@
     gpart[3] = collect(2, cps2)
     cps3 = spread(3)
     arrived(qg2, arsem.at[3])
-    for h in range(HEADS):
-        at = slice(h * HEAD, (h + 1) * HEAD)
-        later = qg2[2 * h:2 * h + 2].reshape(HEAD, HEAD)
+    swaps.append(swap(qg2, qg2, mine, 5))
+    landed(oqg, theirs, 3)
+    first = 1.0 - second
+    for n in range(HEADS):
+        if n == HEADS // 2:
+            landed(qg2, theirs, 5)
+        h = n + (1 - 2 * (n // 8)) * 8 * c
+        at, two = head(h), pl.ds(2 * h, 2)
+        later = (qg2[two].astype(F32) + first * oqg[two].astype(F32)).reshape(HEAD, HEAD).astype(BF)
         gk[:, at] = (scale * (pk[:, at] + dot_nt(vv[:, at], later))).astype(BF)
         gv[:, at] = (scale * (pv[:, at] + dot(kv[:, at], later))).astype(BF)
     gpart[4] = collect(3, cps3)
@@ -455,8 +492,10 @@
         pltpu.make_async_copy(span, span, fsem.at[kind]).wait()
     span = rsend.at[pl.ds(1, DEV - 1)]
     pltpu.make_async_copy(span, span, bsem).wait()
-    for n, buf in enumerate((skv, kvs, sqg, qgs)):
+    for n, buf in enumerate((tkv, kvs, tqg, qgs)):
         arrived(buf, asem.at[n])
+    for cp in swaps:
+        cp.wait_send()
     for cp in store + [gcp] + late:
         cp.wait()
 
@@ -482,14 +521,14 @@
         vm((DEV, 16, 512), BF), vm((DEV, 16, 512), BF),
         vm((TOK, D), F32), vm((TOK, D), BF),
         vm((D, TOK), BF),
-    ] + [vm(state, BF)] * 8 + [
+    ] + [vm(state, BF)] * 6 + [vm((CHIPS, 64, HEAD), BF)] * 6 + [
         vm((HEADS, HEAD, HEAD), BF), vm((TOK, D), F32), vm((TOK, D), F32),
         vm((TOK, D), BF), vm((TOK, D), BF), vm((TOK, D), BF),
         vm((5, 1, D), F32), vm((4, 3, 1, D), F32), vm((1, CAP), F32),
     ]
     dma = pltpu.SemaphoreType.DMA
     sems = [
-        dma((11,)), dma((10,)), dma((2,)), dma((2, 4)), dma, dma((4,)), dma((4,)), dma((4,)), dma((4, 3)), dma((4, 3)),
+        dma((11,)), dma((10,)), dma((2,)), dma((2, 4)), dma, dma((4,)), dma((4,)), dma((4,)), dma((6,)), dma((6,)), dma((4, 3)), dma((4, 3)),
         pltpu.SemaphoreType.REGULAR,
     ]
     return pl.pallas_call(

time: 126 us -> 121 us (0.960)
  Pallas kernels: 125 us -> 120 us
    pallas_call x1, Pallas kernels: 119 us -> 114 us  [call_mega(): pl.pallas_call(functools.partial(mega, scale), out_shape=[jax.ShapeDtypeS...]
where the time goes in v3:
time: 121 us
  Pallas kernels  120 us (99%)
    pallas_call x1, Pallas kernels, call_mega(): pl.pallas_call(functools.partial(mega, scale), out_shape=[jax.ShapeDtypeS...  114 us
    pallas_call x1, Pallas kernels, call_finish(): pl.pallas_call(finish, out_shape=[jax.ShapeDtypeStruct(a, b) for a, b in...  6.33 us

profile of v3, /device:TPU:0, one launch (start us, length us, event | category | flops | bytes accessed | tf_op | source)
XLA Modules:
  0.0 121.1 jit_solution(14916300207387159538)
XLA Ops:
  0.6 114.0 %mega.1 = (bf16[2048,256]{1,0:T(8,128)(2,1)}, bf16[256,2048]{1,0:T(8,128)(2,1)}, bf16[768,256]{1,0:T(8,128)(2,1)}, bf16[256,1536]{1,0:T(8,128)(2,1)}, f32[1,256]...) custom-call(bf16[128,2048]{1,0:T(8,128)(2,1)} %stream_h.1, ...), custom_call_target="tpu_custom_call" | custom-call | tf_op jit(solution)/shard_map/mega/pallas_call | solution.py:534
  114.6 6.3 %finish.1 = (bf16[2048,768]{1,0:T(8,128)(2,1)}, bf16[2048,768]{1,0:T(8,128)(2,1)}, bf16[768,2048]{1,0:T(8,128)(2,1)}, f32[1,256]{1,0:T(1,128)}, bf16[128,2048]{1...) custom-call(bf16[2048,256]{1,0:T(8,128)(2,1)} %get-tuple-element.28., ...), custom_call_target="tpu_custom_call" | custom-call | tf_op jit(solution)/shard_map/finish/pallas_call | solution.py:597

commit v4 on v3

--- a/solution.py
+++ b/solution.py
@@ -115,7 +115,7 @@
             found = jnp.where(eight[r:r + 1, :] == token, 1.0, found)
         return found
 
-    found = lax.fori_loop(0, CAP // 8, match, jnp.zeros((TOK, DEV), F32))
+    found = lax.fori_loop(0, CAP // 8, match, jnp.zeros((TOK, DEV), F32), unroll=2)
     earlier = lax.broadcasted_iota(jnp.int32, (TOK, TOK), 0) > lax.broadcasted_iota(jnp.int32, (TOK, TOK), 1)
     before = dot(jnp.where(earlier, 1.0, 0.0).astype(BF), found.astype(BF))
     code[...] = (found * (before + 1.0)).astype(BF)
@@ -139,7 +139,7 @@
         p8[pl.ds(row0, 256), 128:256] = jnp.where(half == 1, hit, 0.0).astype(BF)
         return carry
 
-    lax.fori_loop(0, 4, build, 0)
+    lax.fori_loop(0, 4, build, 0, unroll=True)
 
     def fold(o):
         o = o.reshape(32, 8, 1024)
@@ -196,7 +196,7 @@
         mixb[h] = jnp.where(tril, dot_nt(qv[:, head(h)], kh), 0.0).astype(BF)
         return carry
 
-    lax.fori_loop(0, HEADS, local_kv, 0)
+    lax.fori_loop(0, HEADS, local_kv, 0, unroll=4)
 
     chip = x * 4 + y
     mine = pl.ds(c * CHIPS, CHIPS)
@@ -224,6 +224,20 @@
             return carry
 
         lax.fori_loop(1, CHIPS, one, 0)
+        dst[base + at] = src[at]
+
+    reach = sorted(
+        [(dx, dy) for dx in range(4) for dy in range(4) if dx + dy],
+        key=lambda o: (-min(o[0], 4 - o[0]) - min(o[1], 4 - o[1]), o[0] + 2 * o[1]),
+    )
+
+    def scatter_far(src, dst, base, at, n):
+        for dx, dy in reach:
+            x2, y2 = rem(x + dx, 4), rem(y + dy, 4)
+            pltpu.make_async_remote_copy(
+                src.at[x2 * 4 + y2], dst.at[base + at], asem.at[n], arsem.at[n],
+                device_id=dev(z, x2 * 8 + y2 * 2 + c), device_id_type=MESH,
+            ).start()
         dst[base + at] = src[at]
 
     def arrived(dst, sem):
@@ -305,7 +319,7 @@
         dpre[:, pl.ds(pl.multiple_of(c0 + FF, 256), 256)] = (gh * silu).astype(BF)
         return carry
 
-    lax.fori_loop(0, 3, front, 0)
+    lax.fori_loop(0, 3, front, 0, unroll=True)
 
     def back(n, carry):
         r0 = pl.multiple_of(n * 256, 256)
@@ -315,7 +329,7 @@
         stacked[pl.ds(h0, 256), pl.ds(c0, 256)] = gr.astype(BF)
         return carry
 
-    lax.fori_loop(0, 8, back, 0)
+    lax.fori_loop(0, 8, back, 0, unroll=4)
 
     def refill(gi, carry):
         r = lax.broadcasted_iota(jnp.int32, (256, 512), 0) + gi * 256
@@ -364,7 +378,7 @@
         kvs[r] = total.astype(BF)
         return total + kv1[r].astype(F32)
 
-    lax.fori_loop(0, CHIPS, prefix, jnp.zeros((64, HEAD), F32))
+    lax.fori_loop(0, CHIPS, prefix, jnp.zeros((64, HEAD), F32), unroll=True)
     scatter(kvs, kv2, c * CHIPS, chip, 1)
 
     for gi in range(4):
@@ -429,7 +443,7 @@
         swaps.append(swap(sqg, oqg, (theirs, mine)[part], 2 + part))
     landed(oqg, mine, 2)
     tqg[...] = (sqg[mine].astype(F32) + oqg[mine].astype(F32)).astype(BF)
-    scatter(tqg, qg1, 0, chip, 2)
+    scatter_far(tqg, qg1, 0, chip, 2)
     arrived(kv2, arsem.at[1])
     swaps.append(swap(kv2, kv2, mine, 4))
     gpart[1] = collect(0, cps0)
@@ -443,7 +457,7 @@
         pv[:, head(h)] = dot_tn(mixb[h], gh)
         return carry
 
-    lax.fori_loop(0, HEADS, local_terms, 0)
+    lax.fori_loop(0, HEADS, local_terms, 0, unroll=4)
     arrived(qg1, arsem.at[2])
 
     def suffix(n, total):
@@ -451,8 +465,8 @@
         qgs[r] = total.astype(BF)
         return total + qg1[r].astype(F32)
 
-    lax.fori_loop(0, CHIPS, suffix, jnp.zeros((64, HEAD), F32))
-    scatter(qgs, qg2, c * CHIPS, chip, 3)
+    lax.fori_loop(0, CHIPS, suffix, jnp.zeros((64, HEAD), F32), unroll=True)
+    scatter_far(qgs, qg2, c * CHIPS, chip, 3)
     gpart[2] = collect(1, cps1)
     cps2 = spread(2)
     landed(okv, theirs, 1)
@@ -465,7 +479,7 @@
         gq[:, head(h)] = (scale * (gin[:, head(h)] + dot_nt(g[:, head(h)], prior))).astype(BF)
         return carry
 
-    lax.fori_loop(0, HEADS, early_terms, 0)
+    lax.fori_loop(0, HEADS, early_terms, 0, unroll=4)
     late = [pltpu.make_async_copy(gq, gq_o, osem.at[5])]
     late[0].start()
     gpart[3] = collect(2, cps2)

time: 121 us -> 120 us (level)
    pallas_call x1, Pallas kernels: 114 us -> 112 us  [call_mega(): pl.pallas_call(functools.partial(mega, scale), out_shape=[jax.ShapeDtypeS...]
where the time goes in v4:
time: 120 us; the launch traced here: 119 us
  Pallas kernels  119 us (99%)
    pallas_call x1, Pallas kernels, call_mega(): pl.pallas_call(functools.partial(mega, scale), out_shape=[jax.ShapeDtypeS...  112 us
    pallas_call x1, Pallas kernels, call_finish(): pl.pallas_call(finish, out_shape=[jax.ShapeDtypeStruct(a, b) for a, b in...  6.33 us

profile of v4, /device:TPU:0, one launch (start us, length us, event | category | flops | bytes accessed | tf_op | source)
XLA Modules:
  0.0 119.4 jit_solution(8287099905561846775)
XLA Ops:
  0.6 112.3 %mega.1 = (bf16[2048,256]{1,0:T(8,128)(2,1)}, bf16[256,2048]{1,0:T(8,128)(2,1)}, bf16[768,256]{1,0:T(8,128)(2,1)}, bf16[256,1536]{1,0:T(8,128)(2,1)}, f32[1,256]...) custom-call(bf16[128,2048]{1,0:T(8,128)(2,1)} %stream_h.1, ...), custom_call_target="tpu_custom_call" | custom-call | tf_op jit(solution)/shard_map/mega/pallas_call | solution.py:548
  112.9 6.3 %finish.1 = (bf16[2048,768]{1,0:T(8,128)(2,1)}, bf16[2048,768]{1,0:T(8,128)(2,1)}, bf16[768,2048]{1,0:T(8,128)(2,1)}, f32[1,256]{1,0:T(1,128)}, bf16[128,2048]{1...) custom-call(bf16[2048,256]{1,0:T(8,128)(2,1)} %get-tuple-element.28., ...), custom_call_target="tpu_custom_call" | custom-call | tf_op jit(solution)/shard_map/finish/pallas_call | solution.py:611

commit v5 on v4

--- a/solution.py
+++ b/solution.py
@@ -62,7 +62,7 @@
     stream_h, cot_h, gain_h, index_h, gates_h, wg_h, wu_h, wd_h, q_h, k_h, v_h,
     rows_o, gout_o, hid_o, dpre_o, router_o, g_o, gq_o, gk_o, gv_o, gain_o,
     stream, cot, gain, index, gates, wg, wu, wd, qv, kv, vv,
-    normed, xin, tindex, code, p8, send, recv, acc, rows, dy, gout, ghid, hid, dpre, rowst, hidt, stacked,
+    normed, xin, tindex, code, p8, p8t, send, recv, acc, rows, dy, gout, ghid, hid, dpre, rowst, hidt, stacked,
     wgt, wut, wdt, rsend, rrecv,
     gin, g, qt, skv, sqg, okv, oqg, kv2, qg2, tkv, kv1, kvs, tqg, qg1, qgs, mixb, pk, pv, gq, gk, gv, gpart, gland, router,
     lsem, osem, fsem, frsem, bsem, brsem, asem, arsem, wsem, wrsem, gsem, grsem, zsem,
@@ -278,6 +278,8 @@
         return carry
 
     lax.fori_loop(0, 8, turn_weights, 0)
+    for n in range(4):
+        p8t[:, n * 256:(n + 1) * 256] = p8[n * 256:(n + 1) * 256, :].T
     landed(okv, mine, 0)
     tkv[...] = (skv[mine].astype(F32) + okv[mine].astype(F32)).astype(BF)
     scatter(tkv, kv1, 0, chip, 0)
@@ -388,7 +390,7 @@
         for half in range(2):
             f = rrecv[pl.ds(gi * 32, 32)].astype(F32).reshape(32, 2, 8, 512)[:, half]
             f = f.reshape(256, 512).astype(BF)
-            part = dot_tn(p8[gi * 256:(gi + 1) * 256, :], f)
+            part = dot(p8t[:, gi * 256:(gi + 1) * 256], f)
             for hh in range(2):
                 c0 = hh * 1024 + half * 512
                 piece = part[hh * TOK:(hh + 1) * TOK, :]
@@ -527,7 +529,7 @@
         vm((TOK, D), BF), vm((TOK, D), BF), vm((1, D), F32), vm((DEV, CAP), jnp.int32), vm((1, CAP), F32),
         vm((D, FF), BF), vm((D, FF), BF), vm((FF, D), BF),
         vm((TOK, D), BF), vm((TOK, D), BF), vm((TOK, D), BF),
-        vm((TOK, D), F32), vm((2, 256, 1024), BF), vm((CAP, DEV), F32), vm((TOK, DEV), BF), vm((1024, 256), BF),
+        vm((TOK, D), F32), vm((2, 256, 1024), BF), vm((CAP, DEV), F32), vm((TOK, DEV), BF), vm((1024, 256), BF), vm((256, 1024), BF),
         vm((2, DEV, 16, 512), BF), vm((2, DEV, 16, 512), BF), vm((512, 1024), F32), vm((CAP, D), BF),
         vm((CAP, D), BF), vm((CAP, D), BF), vm((CAP, FF), F32), vm((CAP, FF), BF), vm((CAP, 2 * FF), BF),
         vm((D, CAP), BF), vm((FF, CAP), BF), vm((512, 1024), BF),

time: 120 us -> 120 us (level)
  no operation moved by 1% of the time
where the time goes in v5:
time: 120 us; the launch traced here: 119 us
  Pallas kernels  119 us (99%)
    pallas_call x1, Pallas kernels, call_mega(): pl.pallas_call(functools.partial(mega, scale), out_shape=[jax.ShapeDtypeS...  112 us
    pallas_call x1, Pallas kernels, call_finish(): pl.pallas_call(finish, out_shape=[jax.ShapeDtypeStruct(a, b) for a, b in...  6.33 us

profile of v5, /device:TPU:0, one launch (start us, length us, event | category | flops | bytes accessed | tf_op | source)
XLA Modules:
  0.0 119.4 jit_solution(7437727799319703790)
XLA Ops:
  0.6 112.3 %mega.1 = (bf16[2048,256]{1,0:T(8,128)(2,1)}, bf16[256,2048]{1,0:T(8,128)(2,1)}, bf16[768,256]{1,0:T(8,128)(2,1)}, bf16[256,1536]{1,0:T(8,128)(2,1)}, f32[1,256]...) custom-call(bf16[128,2048]{1,0:T(8,128)(2,1)} %stream_h.1, ...), custom_call_target="tpu_custom_call" | custom-call | tf_op jit(solution)/shard_map/mega/pallas_call | solution.py:550
  112.9 6.3 %finish.1 = (bf16[2048,768]{1,0:T(8,128)(2,1)}, bf16[2048,768]{1,0:T(8,128)(2,1)}, bf16[768,2048]{1,0:T(8,128)(2,1)}, f32[1,256]{1,0:T(1,128)}, bf16[128,2048]{1...) custom-call(bf16[2048,256]{1,0:T(8,128)(2,1)} %get-tuple-element.28., ...), custom_call_target="tpu_custom_call" | custom-call | tf_op jit(solution)/shard_map/finish/pallas_call | solution.py:613
